TPU v7x, 512 devices: a whole 4x8x8 slice. The times are simulated.
512 devices in a mesh: head: 16 (over y, core), seq: 32 (over x, z).
Axes of the slice: x: 4, y: 8, z: 8, core: 2. Of those that a mesh axis runs over, the one named last changes fastest.
Arguments:
- layer_input: bfloat16 [4096, 4096], P('seq', 'head'), may hold values from -6 to 6
- receptance: bfloat16 [4096, 4096], P('seq', 'head'), may hold values from -6 to 6
- key_act: bfloat16 [4096, 4096], P('seq', 'head'), may hold values from -0.75 to 0.75
- value_act: bfloat16 [4096, 4096], P('seq', 'head'), may hold values from -6 to 6
- attention_result_sensitivity: bfloat16 [4096, 4096], P('seq', 'head'), may hold values from -0.625 to 0.625
- time_first: float32 [64, 64], P('head'), may hold values from -1 to 1
- decay_exponent_base: float32 [4096], P('head'), may hold values from -9 to -3.4
- decay_shift_mix: float32 [4096], P('head'), may hold values from 0 to 1
- mix_rkv: float32 [3, 4096], replicated, may hold values from 0 to 1
- decay_adapter_down: float32 [4096, 128], P('head'), may hold values from -0.09375 to 0.09375
- decay_adapter_up: float32 [128, 4096], P(None, 'head'), may hold values from -1 to 1
- proj_weights: bfloat16 [3, 4096, 4096], P(None, 'seq', 'head'), may hold values from -0.09375 to 0.09375
Outputs:
- stratum_source_sensitivity: bfloat16 [4096, 4096], P('seq', 'head')
- decay_down_grad: float32 [4096, 128], P('head')
- decay_up_grad: float32 [128, 4096], P(None, 'head')
- decay_base_grad: float32 [4096], P('head')
- time_first_grad: float32 [64, 64], P('head')
All inputs are finite; a program needn't handle non-finite values.
Results may differ from a plain program's by a relative error of at most 0.018.
Values may be sent and summed in bfloat16 or wider, within the bound.
A program may use at most 64 MiB of HBM per device.

v0:
```python
from functools import partial

import jax
import jax.numpy as jnp
from jax import lax
from jax.sharding import PartitionSpec as P

BLOCK = 32


EXACT_ARITHMETIC = lax.Precision.HIGHEST


def shifted(block, axis, distance):
    devices = range(lax.axis_size(axis))
    route = [(i - distance, i) for i in devices if i - distance in devices]
    return lax.ppermute(block, axis, route)


def gathered_total(array, axis):
    return lax.all_gather(array, axis).sum(0)


def sent_to_all(array, axis):
    copies = jnp.broadcast_to(array, (lax.axis_size(axis), *array.shape))
    return lax.all_to_all(copies, axis, split_axis=0, concat_axis=0, tiled=True)


def joined_along(blocks, dim):
    blocks = jnp.moveaxis(blocks, 0, dim)
    dims = blocks.shape
    return blocks.reshape(*dims[:dim], dims[dim] * dims[dim + 1], *dims[dim + 2 :])


def collect(array, axis, dim):
    blocks = sent_to_all(array, axis)
    return joined_along(blocks, dim)


def in_one_piece(arrays, axis, dim, along):
    widths = [a.shape[along] for a in arrays]
    both = jnp.concatenate(arrays, axis=along)
    out = lax.all_gather(both, axis, axis=dim, tiled=True)
    return tuple(jnp.split(out, [sum(widths[:k]) for k in range(1, len(widths))], axis=along))


def piecewise(array, axis, dim, apply, out_dim):
    size, width = (lax.axis_size(axis), array.shape[dim])
    count = 2 if width % 2 == 0 else 1
    finished, length = ([], width // count)
    for k in range(count):
        section = lax.slice_in_dim(array, k * length, (k + 1) * length, axis=dim)
        starts = jnp.arange(size) * width + k * length
        finished.append(jax.vmap(apply)(lax.all_gather(section, axis), starts))
    return joined_along(jnp.concatenate(finished, axis=out_dim + 1), out_dim)


def cut_along(array, dim, count):
    dims = array.shape
    blocks = array.reshape(*dims[:dim], count, dims[dim] // count, *dims[dim + 1 :])
    return jnp.moveaxis(blocks, dim, 0)


def summed_on_arrival(array, axis, dim):
    blocks = cut_along(array, dim, lax.axis_size(axis))
    arrived = lax.all_to_all(blocks, axis, split_axis=0, concat_axis=0, tiled=True)
    return arrived.astype(jnp.float32).sum(axis=0)


def block_terms(gate_matrix, lookup_matrix, payload_matrix, grads_out, fading_natural_scale):
    cumul = jnp.cumsum(fading_natural_scale, axis=1)
    before = cumul - fading_natural_scale
    final = cumul[:, -1]
    to_end = jnp.exp(final[:, None] - cumul)
    state_part = jnp.einsum(
        "bshi,bshj->bhij", lookup_matrix * to_end, payload_matrix, precision=EXACT_ARITHMETIC
    )
    grad_part = jnp.einsum(
        "bshi,bshj->bhij", gate_matrix * jnp.exp(before), grads_out, precision=EXACT_ARITHMETIC
    )
    return (cumul, before, final, state_part, grad_part)


def sensitivity_each_segment(initial_reward, sequence_entries):
    (
        gate_matrix,
        lookup_matrix,
        payload_matrix,
        grads_out,
        cumul,
        before,
        final,
        state_in,
        grad_in,
        state_part,
    ) = sequence_entries
    length = gate_matrix.shape[0]
    positions = jnp.arange(length)
    lower = positions[:, None] > positions[None, :]
    strict_up = (positions[:, None] < positions[None, :]).astype(jnp.float32)
    upper = (positions[:, None] <= positions[None, :]).astype(jnp.float32)
    spread = jnp.where(lower[:, :, None, None], before[:, None] - cumul[None, :], -jnp.inf)
    decays = jnp.exp(spread)
    pairs = jnp.einsum("thj,shj->tsh", grads_out, payload_matrix, precision=EXACT_ARITHMETIC)
    scores = jnp.einsum(
        "tshi,thi,shi->tsh", decays, gate_matrix, lookup_matrix, precision=EXACT_ARITHMETIC
    )
    to_end = jnp.exp(final[None] - cumul)
    gate_memory_product = jnp.einsum(
        "tshi,tsh,shi->thi", decays, pairs, lookup_matrix, precision=EXACT_ARITHMETIC
    )
    gate_memory_product = gate_memory_product + jnp.exp(before) * jnp.einsum(
        "hij,thj->thi", state_in, grads_out, precision=EXACT_ARITHMETIC
    )
    cumulative_lookup_memory = jnp.einsum(
        "tshi,tsh,thi->shi", decays, pairs, gate_matrix, precision=EXACT_ARITHMETIC
    )
    cumulative_lookup_memory = cumulative_lookup_memory + to_end * jnp.einsum(
        "hij,shj->shi", grad_in, payload_matrix, precision=EXACT_ARITHMETIC
    )
    val_state = jnp.einsum("tsh,thj->shj", scores, grads_out, precision=EXACT_ARITHMETIC)
    val_state = val_state + jnp.einsum(
        "shi,hij->shj", lookup_matrix * to_end, grad_in, precision=EXACT_ARITHMETIC
    )
    self_pair_contribution = jnp.sum(grads_out * payload_matrix, -1)[..., None]
    scaled_contributions = jnp.sum(gate_matrix * initial_reward * lookup_matrix, -1)[..., None]
    gate_sensitivity = gate_memory_product + initial_reward * lookup_matrix * self_pair_contribution
    lookup_sensitivity = (
        cumulative_lookup_memory + initial_reward * gate_matrix * self_pair_contribution
    )
    payload_sensitivity = val_state + scaled_contributions * grads_out
    reward_sensitivity = jnp.sum(gate_matrix * lookup_matrix * self_pair_contribution, 0)
    state_out = jnp.exp(final)[..., None] * state_in + state_part
    at_end = jnp.sum(grad_in * state_out, -1)
    fading_scale_sensitivity = jnp.einsum(
        "ts,shi->thi", strict_up, gate_matrix * gate_memory_product, precision=EXACT_ARITHMETIC
    )
    fading_scale_sensitivity = (
        fading_scale_sensitivity
        - jnp.einsum(
            "ts,shi->thi",
            upper,
            lookup_matrix * cumulative_lookup_memory,
            precision=EXACT_ARITHMETIC,
        )
        + at_end[None]
    )
    return (
        gate_sensitivity,
        lookup_sensitivity,
        payload_sensitivity,
        fading_scale_sensitivity,
        reward_sensitivity,
    )


def per_device(
    layer_input,
    receptance,
    key_act,
    value_act,
    attention_result_sensitivity,
    time_first,
    decay_exponent_base,
    decay_shift_mix,
    mix_rkv,
    decay_adapter_down,
    decay_adapter_up,
    proj_weights,
):
    tok_rows, group_columns = layer_input.shape
    heads_dev, head_size = time_first.shape
    features = layer_input.astype(jnp.float32)
    carried_row = shifted(layer_input[tok_rows - 1 :], "seq", 1).astype(jnp.float32)
    previous = jnp.concatenate([carried_row, features[:-1]], 0)
    decay_input = features + decay_shift_mix * (previous - features)
    adapter_preactivation = gathered_total(
        jnp.dot(decay_input, decay_adapter_down, precision=EXACT_ARITHMETIC), "head"
    )
    adapter_middle = jnp.tanh(adapter_preactivation)
    fading_natural_scale = -jnp.exp(
        decay_exponent_base + jnp.dot(adapter_middle, decay_adapter_up, precision=EXACT_ARITHMETIC)
    )
    count = tok_rows // BLOCK

    def blocked(array):
        return array.astype(jnp.float32).reshape(count, BLOCK, heads_dev, head_size)

    gate_matrix = blocked(receptance)
    lookup_matrix = blocked(key_act)
    payload_matrix = blocked(value_act)
    grads_out = blocked(attention_result_sensitivity)
    cumul, before, final, state_part, grad_part = block_terms(
        gate_matrix, lookup_matrix, payload_matrix, grads_out, blocked(fading_natural_scale)
    )
    zero_state = jnp.zeros((heads_dev, head_size, head_size), jnp.float32)
    zero_decay = jnp.zeros((heads_dev, head_size), jnp.float32)

    def carry_step(carry, sequence_entries):
        running, decay_sum = carry
        block_final, block_term = sequence_entries
        updated = (jnp.exp(block_final)[..., None] * running + block_term, decay_sum + block_final)
        return (updated, (running, decay_sum))

    (local_state, device_decay), (starts_local, starts_decay) = lax.scan(
        carry_step, (zero_state, zero_decay), (final, state_part)
    )
    (local_grad, unused), (ends_local, ends_decay) = lax.scan(
        carry_step, (zero_state, zero_decay), (final, grad_part), reverse=True
    )
    totals = collect(device_decay[None], "seq", 0)
    prefix = jnp.cumsum(totals, 0) - totals
    mine = lax.axis_index("seq")
    own_prefix = lax.dynamic_index_in_dim(prefix, mine, 0, keepdims=False)
    own_total = lax.dynamic_index_in_dim(totals, mine, 0, keepdims=False)
    state_piece, grad_piece = in_one_piece((local_state[None], local_grad[None]), "seq", 0, 1)
    number = state_piece.shape[0]
    ranks = jnp.arange(number)
    forward_gap = jnp.minimum(own_prefix[None] - prefix - totals, 0.0)
    backward_gap = jnp.minimum(prefix - own_prefix[None] - own_total[None], 0.0)
    forward_weight = jnp.where((ranks < mine)[:, None, None], jnp.exp(forward_gap), 0.0)
    backward_weight = jnp.where((ranks > mine)[:, None, None], jnp.exp(backward_gap), 0.0)
    forward_acc = jnp.einsum(
        "nhi,nhij->hij", forward_weight, state_piece, precision=EXACT_ARITHMETIC
    )
    backward_acc = jnp.einsum(
        "nhi,nhij->hij", backward_weight, grad_piece, precision=EXACT_ARITHMETIC
    )
    starts = starts_local + jnp.exp(starts_decay)[..., None] * forward_acc[None]
    ends = ends_local + jnp.exp(ends_decay)[..., None] * backward_acc[None]
    (
        gate_sensitivity,
        lookup_sensitivity,
        payload_sensitivity,
        fading_scale_sensitivity,
        reward_each_segment,
    ) = lax.map(
        partial(sensitivity_each_segment, time_first),
        (
            gate_matrix,
            lookup_matrix,
            payload_matrix,
            grads_out,
            cumul,
            before,
            final,
            starts,
            ends,
            state_part,
        ),
    )
    device_reward = jnp.sum(reward_each_segment, 0)

    def flatten(array):
        return array.reshape(tok_rows, group_columns)

    preactivation_gradient = flatten(fading_scale_sensitivity) * fading_natural_scale
    device_raising_matrix = jnp.dot(
        adapter_middle.T, preactivation_gradient, precision=EXACT_ARITHMETIC
    )
    device_fading_floor = jnp.sum(preactivation_gradient, 0)
    middle_gradient = gathered_total(
        jnp.dot(preactivation_gradient, decay_adapter_up.T, precision=EXACT_ARITHMETIC), "head"
    ) * (1.0 - adapter_middle * adapter_middle)
    down_local = jnp.dot(decay_input.T, middle_gradient, precision=EXACT_ARITHMETIC)
    (
        lowering_matrix_sensitivity,
        raising_matrix_sensitivity,
        floor_rate_sensitivity,
        reward_sensitivity,
    ) = lax.psum((down_local, device_raising_matrix, device_fading_floor, device_reward), "seq")
    decay_input_gradient = jnp.dot(
        middle_gradient, decay_adapter_down.T, precision=EXACT_ARITHMETIC
    )
    projected = jnp.stack(
        [flatten(gate_sensitivity), flatten(lookup_sensitivity), flatten(payload_sensitivity)]
    ).astype(jnp.bfloat16)

    def project(piece, start):
        mixes = lax.dynamic_slice_in_dim(mix_rkv, start, piece.shape[1], 1)
        terms = jnp.einsum("mtc,mnc->mtn", projected, piece, preferred_element_type=jnp.float32)
        own_piece = jnp.sum((1.0 - mixes)[:, None, :] * terms, 0)
        prior_piece = jnp.sum(mixes[:, None, :] * terms, 0)
        return jnp.stack([own_piece, prior_piece])

    gradient_portions = piecewise(proj_weights, "seq", 1, project, 2)
    token_offset = lax.axis_index("head") * group_columns
    adapter_terms = jnp.stack(
        [(1.0 - decay_shift_mix) * decay_input_gradient, decay_shift_mix * decay_input_gradient]
    )
    current_token = lax.dynamic_slice_in_dim(gradient_portions, token_offset, group_columns, 2)
    gradient_portions = lax.dynamic_update_slice_in_dim(
        gradient_portions, current_token + adapter_terms, token_offset, 2
    )
    own_portion = gradient_portions[0]
    previous_portion = gradient_portions[1]
    next_first = shifted(previous_portion[0:1], "seq", -1)
    group_term = own_portion + jnp.concatenate([previous_portion[1:], next_first], 0)
    stratum_source_sensitivity = summed_on_arrival(
        group_term.astype(jnp.bfloat16), "head", 1
    ).astype(jnp.bfloat16)
    return (
        stratum_source_sensitivity,
        lowering_matrix_sensitivity,
        raising_matrix_sensitivity,
        floor_rate_sensitivity,
        reward_sensitivity,
    )


def solution(mesh):
    return jax.shard_map(
        per_device,
        mesh=mesh,
        in_specs=(
            P("seq", "head"),
            P("seq", "head"),
            P("seq", "head"),
            P("seq", "head"),
            P("seq", "head"),
            P("head", None),
            P("head"),
            P("head"),
            P(),
            P("head", None),
            P(None, "head"),
            P(None, "seq", "head"),
        ),
        out_specs=(P("seq", "head"), P("head", None), P(None, "head"), P("head"), P("head", None)),
        check_vma=False,
    )
```

profile of v0, /device:TPU:6, one launch (start us, length us, event | category | flops | bytes accessed | tf_op | source)
XLA Modules:
  0.0 587.8 jit_solution(2083734306064413648)
XLA Ops:
  8.0 4.3 collective-permute-start
  13.1 7.6 %collective-permute-done = bf16[1,256]{1,0:T(2,128)(2,1)S(1)} collective-permute-done((bf16[1,256]{1,0:T(2,128)(2,1)S(1)}, bf16[1,256]{1,0:T(2,128)(2,1)S(1)}, u32[]{:S(2)}, u32[]{:S(2)}) %collective-permute-start) | collective-permute-done | bytes 544 | tf_op jit(solution)/shard_map/ppermute | solution.py:17
  27.9 34.6 %all-gather.12.cloned.1.call-done = f32[2048,128]{1,0:T(8,128)} async-done(((f32[128,128]{1,0:T(8,128)}), f32[2048,128]{1,0:T(8,128)}) %all-gather.12.cloned.1.call-update) | async-done | bytes 1048592 | tf_op jit(solution)/shard_map/all_gather | solution.py:21
  69.2 3.4 while.62
  74.9 63.7 %while.59 = (s32[]{:T(128)}, f32[3,4096]{1,0:T(4,128)}, s32[32,2]{0,1:T(2,128)S(1)}, f32[32,3,64]{2,1,0:T(4,128)S(1)}, s32[]{:T(128)}) while((s32[]{:T(128)}, f32[3,4096]{1,0:T(4,128)}, s32[32,2]{0,1:T(2,128)S(1)}, f32[32,3,64]{2,1,0:T(4,128)S(1)}, s32[]{:T(128)}) %tuple.136), condition=%wide.while_cond, body=%wide.while_body.sunk | while | flops 2 | bytes 2913 | solution.py:280
  139.3 64.2 %while.60 = (s32[]{:T(128)}, f32[3,4096]{1,0:T(4,128)}, s32[32,2]{0,1:T(2,128)S(1)}, f32[32,3,64]{2,1,0:T(4,128)S(1)}, s32[]{:T(128)}) while((s32[]{:T(128)}, f32[3,4096]{1,0:T(4,128)}, s32[32,2]{0,1:T(2,128)S(1)}, f32[32,3,64]{2,1,0:T(4,128)S(1)}, s32[]{:T(128)}) %tuple.158), condition=%wide.while_cond.1, body=%wide.while_body.1.sunk | while | flops 2 | bytes 2913 | solution.py:280
  204.2 10.5 %all-to-all-start = ((f32[32,1,256]{2,1,0:T(1,128)}), f32[32,1,256]{2,1,0:T(1,128)S(1)}, u32[]{:S(2)}, u32[]{:S(2)}) async-start(f32[32,1,256]{2,1,0:T(1,128)} %reshape.226), calls=%async_computation | async-start | bytes 65536 | tf_op jit(solution)/shard_map/all_to_all | solution.py:26
  216.2 6.6 %all-to-all-done = f32[32,1,256]{2,1,0:T(1,128)S(1)} async-done(((f32[32,1,256]{2,1,0:T(1,128)}), f32[32,1,256]{2,1,0:T(1,128)S(1)}, u32[]{:S(2)}, u32[]{:S(2)}) %all-to-all-start) | async-done | bytes 32800 | tf_op jit(solution)/shard_map/all_to_all | solution.py:26
  224.6 4.3 fusion.93
  228.9 5.7 fusion.44
  234.6 5.9 %fusion.46 = f32[4,64,1,64]{3,2,1,0:T(1,128)S(1)} fusion(f32[32,4,64,1]{0,3,2,1:T(1,128)S(1)} %copy.136, f32[32,4,64,64]{3,2,1,0:T(8,128)S(1)} %get-tuple-element.529), kind=kOutput, calls=%fused_computation.98 | convolution fusion | flops 6291456 | bytes 2195456 | tf_op jit(solution)/shard_map/nhi,nhij->hij/dot_general | solution.py:223
  242.3 95.5 %while.58 = (s32[]{:T(128)}, bf16[4,32,4,64]{3,1,2,0:T(8,128)(2,1)}, bf16[4,32,4,64]{3,1,2,0:T(8,128)(2,1)}, bf16[4,32,4,64]{3,1,2,0:T(8,128)(2,1)}, f32[4,32,4,...) while((s32[]{:T(128)}, ...), condition=%wide.region_12.13_spmd, body=%wide.region_7.12_spmd.sunk | while | flops 38292032 | bytes 9019765 | solution.py:237
  252.2 2.8 multiply_reduce_fusion.7
  257.8 4.5 fusion.134
  276.1 2.8 multiply_reduce_fusion.7
  281.6 4.5 fusion.134
  300.0 2.8 multiply_reduce_fusion.7
  305.5 4.5 fusion.134
  323.8 2.8 multiply_reduce_fusion.7
  329.4 4.5 fusion.134
  345.8 3.5 fusion.50
  349.5 3.5 fusion.48
  355.5 5.6 copy.143
  361.2 25.1 %all-gather.18.cloned.1.call-done = f32[2048,128]{1,0:T(8,128)} async-done(((f32[128,128]{1,0:T(8,128)}), f32[2048,128]{1,0:T(8,128)}) %all-gather.18.cloned.1.call-update) | async-done | bytes 1048592 | tf_op jit(solution)/shard_map/all_gather | solution.py:21
  390.5 6.4 %collective-permute-start.1 = (f32[1,4096]{1,0:T(1,128)S(1)}, f32[1,4096]{1,0:T(1,128)S(1)}, u32[]{:S(2)}, u32[]{:S(2)}) collective-permute-start(f32[1,4096]{1,0:T(1,128)S(1)} %slice_bitcast_fusion), channel_id=1, source_target_pairs={{1,0},{2,1},{3,2},{4,3},{5,4},{6,5},{7,6},{8,7},{9,8},{10,9},{11,1... | collective-permute-start | bytes 49160 | tf_op jit(solution)/shard_map/ppermute | solution.py:17
  396.9 3.1 slice.64
  403.5 3.0 copy.113
  407.6 3.3 concatenate.33
  410.9 3.8 fusion.59
  414.7 4.7 all-to-all-start.1
  421.6 61.8 %all-reduce.2 = (f32[256]{0:T(256)}, f32[4,64]{1,0:T(4,128)}) all-reduce(f32[256]{0:T(256)S(1)} %multiply_reduce_fusion.3, f32[4,64]{1,0:T(4,128)S(1)} %reduce_sum.128), channel_id=1, replica_groups=mesh['head'=16,'seq'=32] {'seq'}, use_global_device_ids=true, to_apply=%region_22.23 | all-reduce | flops 512 | bytes 4096 | tf_op jit(solution)/shard_map/psum | solution.py:271
  484.3 93.5 %all-reduce.6.cloned.1.call-done = (f32[256,128]{1,0:T(8,128)}, f32[128,256]{1,0:T(8,128)}) async-done(((f32[256,128]{1,0:T(8,128)}, f32[128,256]{1,0:T(8,128)}), (f32[256,128]{1,0:T(8,128)}, f32[128,256]{1,0:T(8,128)})) %all-reduce.6.cloned.1.call-update) | async-done | bytes 262160 | tf_op jit(solution)/shard_map/psum | solution.py:271
  (558 shorter events, 246.5 us)
Async XLA Ops:
  7.2 14.2 %copy-start = (f32[256,128]{1,0:T(8,128)S(1)}, f32[256,128]{1,0:T(8,128)}, u32[]{:S(2)}) copy-start(f32[256,128]{1,0:T(8,128)} %param.27) | copy-start | bytes 393220
  7.2 56.6 %copy-start.27 = (f32[256]{0:T(256)S(1)}, f32[256]{0:T(256)}, u32[]{:S(2)}) copy-start(f32[256]{0:T(256)} %param.24) | copy-start | bytes 3076
  7.2 56.6 %copy-start.15 = (f32[128,256]{1,0:T(8,128)S(1)}, f32[128,256]{1,0:T(8,128)}, u32[]{:S(2)}) copy-start(f32[128,256]{1,0:T(8,128)} %param.28) | copy-start | bytes 393220
  7.2 55.3 %all-gather.12.cloned.1.call-start = ((), (), s32[]{:S(2)}) async-start(), calls=%async_computation.3 | async-start | bytes 1114112 | tf_op jit(solution)/shard_map/all_gather | solution.py:21
  8.0 12.7 %collective-permute-start = (bf16[1,256]{1,0:T(2,128)(2,1)S(1)}, bf16[1,256]{1,0:T(2,128)(2,1)S(1)}, u32[]{:S(2)}, u32[]{:S(2)}) collective-permute-start(bf16[1,256]{1,0:T(2,128)(2,1)S(1)} %slice.31), channel_id=1, source_target_pairs={{0,1},{1,2},{2,3},{3,4},{4,5},{5,6},{6,7},{7,8},{8,9},{9,10},{10,1... | collective-permute-start | bytes 1544 | tf_op jit(solution)/shard_map/ppermute | solution.py:17
  13.1 7.6 %copy-start.10 = (f32[127,256]{1,0:T(8,128)}, f32[127,256]{1,0:T(8,128)S(1)}, u32[]{:S(2)}) copy-start(f32[127,256]{1,0:T(8,128)S(1)} %slice.62) | copy-start | bytes 390148
  23.1 201.5 %all-gather.10.cloned.1.call-start = ((), (), s32[]{:S(2)}) async-start(), calls=%async_computation.2 | async-start | bytes 8650752 | tf_op jit(solution)/shard_map/all_gather | solution.py:43
  73.4 272.4 %all-gather.14.cloned.1.call-start = ((), (), s32[]{:S(2)}) async-start(), calls=%async_computation.4 | async-start | bytes 3244032 | tf_op jit(solution)/shard_map/all_gather | solution.py:54
  74.2 275.3 %all-gather.16.cloned.1.call-start = ((), (), s32[]{:S(2)}) async-start(), calls=%async_computation.5 | async-start | bytes 3244032 | tf_op jit(solution)/shard_map/all_gather | solution.py:54
  138.6 84.7 %copy-start.13 = (f32[32,3,64]{2,1,0:T(4,128)}, f32[32,3,64]{2,1,0:T(4,128)S(1)}, u32[]{:S(2)}) copy-start(f32[32,3,64]{2,1,0:T(4,128)S(1)} %get-tuple-element.298) | copy-start | bytes 73732
  203.5 25.4 %copy-start.14 = (f32[32,3,64]{2,1,0:T(4,128)}, f32[32,3,64]{2,1,0:T(4,128)S(1)}, u32[]{:S(2)}) copy-start(f32[32,3,64]{2,1,0:T(4,128)S(1)} %get-tuple-element.306) | copy-start | bytes 73732
  204.2 18.6 %all-to-all-start = ((f32[32,1,256]{2,1,0:T(1,128)}), f32[32,1,256]{2,1,0:T(1,128)S(1)}, u32[]{:S(2)}, u32[]{:S(2)}) async-start(f32[32,1,256]{2,1,0:T(1,128)} %reshape.226), calls=%async_computation | async-start | bytes 65536 | tf_op jit(solution)/shard_map/all_to_all | solution.py:26
  214.7 171.5 %all-gather.18.cloned.1.call-start = ((), (), s32[]{:S(2)}) async-start(), calls=%async_computation.6 | async-start | bytes 1114112 | tf_op jit(solution)/shard_map/all_gather | solution.py:21
  257.7 8.4 %copy-start.4 = (f32[4,32,4,64]{3,2,1,0:T(4,128)S(1)}, f32[4,32,4,64]{3,2,1,0:T(4,128)}, u32[]{:S(2)}) copy-start(f32[4,32,4,64]{3,2,1,0:T(4,128)} %copy-done.3) | copy-start | bytes 393220 | tf_op jit(solution)/shard_map/while
  257.7 8.4 %copy-start.7 = (f32[4,32,4,64]{3,2,1,0:T(4,128)S(1)}, f32[4,32,4,64]{3,2,1,0:T(4,128)}, u32[]{:S(2)}) copy-start(f32[4,32,4,64]{3,2,1,0:T(4,128)} %copy-done.6) | copy-start | bytes 393220 | tf_op jit(solution)/shard_map/while
  257.8 8.4 %copy-start.9 = (f32[4,32,4,64]{3,2,1,0:T(4,128)S(1)}, f32[4,32,4,64]{3,2,1,0:T(4,128)}, u32[]{:S(2)}) copy-start(f32[4,32,4,64]{3,2,1,0:T(4,128)} %copy-done.8) | copy-start | bytes 393220 | tf_op jit(solution)/shard_map/while
  281.6 8.5 %copy-start.4 = (f32[4,32,4,64]{3,2,1,0:T(4,128)S(1)}, f32[4,32,4,64]{3,2,1,0:T(4,128)}, u32[]{:S(2)}) copy-start(f32[4,32,4,64]{3,2,1,0:T(4,128)} %copy-done.3) | copy-start | bytes 393220 | tf_op jit(solution)/shard_map/while
  281.6 8.5 %copy-start.7 = (f32[4,32,4,64]{3,2,1,0:T(4,128)S(1)}, f32[4,32,4,64]{3,2,1,0:T(4,128)}, u32[]{:S(2)}) copy-start(f32[4,32,4,64]{3,2,1,0:T(4,128)} %copy-done.6) | copy-start | bytes 393220 | tf_op jit(solution)/shard_map/while
  281.6 8.5 %copy-start.9 = (f32[4,32,4,64]{3,2,1,0:T(4,128)S(1)}, f32[4,32,4,64]{3,2,1,0:T(4,128)}, u32[]{:S(2)}) copy-start(f32[4,32,4,64]{3,2,1,0:T(4,128)} %copy-done.8) | copy-start | bytes 393220 | tf_op jit(solution)/shard_map/while
  305.5 8.4 %copy-start.4 = (f32[4,32,4,64]{3,2,1,0:T(4,128)S(1)}, f32[4,32,4,64]{3,2,1,0:T(4,128)}, u32[]{:S(2)}) copy-start(f32[4,32,4,64]{3,2,1,0:T(4,128)} %copy-done.3) | copy-start | bytes 393220 | tf_op jit(solution)/shard_map/while
  305.5 8.4 %copy-start.7 = (f32[4,32,4,64]{3,2,1,0:T(4,128)S(1)}, f32[4,32,4,64]{3,2,1,0:T(4,128)}, u32[]{:S(2)}) copy-start(f32[4,32,4,64]{3,2,1,0:T(4,128)} %copy-done.6) | copy-start | bytes 393220 | tf_op jit(solution)/shard_map/while
  305.5 8.4 %copy-start.9 = (f32[4,32,4,64]{3,2,1,0:T(4,128)S(1)}, f32[4,32,4,64]{3,2,1,0:T(4,128)}, u32[]{:S(2)}) copy-start(f32[4,32,4,64]{3,2,1,0:T(4,128)} %copy-done.8) | copy-start | bytes 393220 | tf_op jit(solution)/shard_map/while
  329.3 8.5 %copy-start.4 = (f32[4,32,4,64]{3,2,1,0:T(4,128)S(1)}, f32[4,32,4,64]{3,2,1,0:T(4,128)}, u32[]{:S(2)}) copy-start(f32[4,32,4,64]{3,2,1,0:T(4,128)} %copy-done.3) | copy-start | bytes 393220 | tf_op jit(solution)/shard_map/while
  329.3 8.5 %copy-start.7 = (f32[4,32,4,64]{3,2,1,0:T(4,128)S(1)}, f32[4,32,4,64]{3,2,1,0:T(4,128)}, u32[]{:S(2)}) copy-start(f32[4,32,4,64]{3,2,1,0:T(4,128)} %copy-done.6) | copy-start | bytes 393220 | tf_op jit(solution)/shard_map/while
  329.3 8.5 %copy-start.9 = (f32[4,32,4,64]{3,2,1,0:T(4,128)S(1)}, f32[4,32,4,64]{3,2,1,0:T(4,128)}, u32[]{:S(2)}) copy-start(f32[4,32,4,64]{3,2,1,0:T(4,128)} %copy-done.8) | copy-start | bytes 393220 | tf_op jit(solution)/shard_map/while
  337.8 7.7 %copy-start.19 = (bf16[4,32,4,64]{3,1,2,0:T(8,128)(2,1)S(1)}, bf16[4,32,4,64]{3,1,2,0:T(8,128)(2,1)}, u32[]{:S(2)}) copy-start(bf16[4,32,4,64]{3,1,2,0:T(8,128)(2,1)} %get-tuple-element.288) | copy-start | bytes 196612
  337.9 7.9 %copy-start.20 = (f32[32,3,64]{2,0,1:T(8,128)S(1)}, f32[32,3,64]{2,0,1:T(8,128)}, u32[]{:S(2)}) copy-start(f32[32,3,64]{2,0,1:T(8,128)} %copy.107) | copy-start | bytes 73732
  355.5 32.0 %copy-start.24 = (f32[256]{0:T(256)S(1)}, f32[256]{0:T(256)}, u32[]{:S(2)}) copy-start(f32[256]{0:T(256)} %param.25) | copy-start | bytes 3076
  390.5 9.6 %copy-start.1 = (f32[2,128,4096]{2,1,0:T(8,128)S(1)}, f32[2,128,4096]{2,1,0:T(8,128)}, u32[]{:S(2)}) copy-start(f32[2,128,4096]{2,1,0:T(8,128)} %fusion.60) | copy-start | bytes 12582916
  390.5 15.9 %collective-permute-start.1 = (f32[1,4096]{1,0:T(1,128)S(1)}, f32[1,4096]{1,0:T(1,128)S(1)}, u32[]{:S(2)}, u32[]{:S(2)}) collective-permute-start(f32[1,4096]{1,0:T(1,128)S(1)} %slice_bitcast_fusion), channel_id=1, source_target_pairs={{1,0},{2,1},{3,2},{4,3},{5,4},{6,5},{7,6},{8,7},{9,8},{10,9},{11,1... | collective-permute-start | bytes 49160 | tf_op jit(solution)/shard_map/ppermute | solution.py:17
  414.7 68.7 %all-to-all-start.1 = ((bf16[16,128,256]{1,2,0:T(8,128)(2,1)}), bf16[16,128,256]{1,2,0:T(8,128)(2,1)S(1)}, u32[]{:S(2)}, u32[]{:S(2)}) async-start(bf16[16,128,256]{1,2,0:T(8,128)(2,1)} %fusion.59), calls=%async_computation.1 | async-start | bytes 2097152 | tf_op jit(solution)/shard_map/all_to_all | solution.py:66
  419.5 158.4 %all-reduce.6.cloned.1.call-start = ((), (), s32[]{:S(2)}) async-start(), calls=%async_computation.7 | async-start | bytes 524288 | tf_op jit(solution)/shard_map/psum | solution.py:271
  (24 other events, 73.7 us)
Sparse Core Ops, SparseCore 0:
  23.2 39.1 all-gather.11
  73.5 101.3 all-gather.9
  178.1 82.4 all-gather.13
  263.6 82.0 all-gather.15
  347.6 38.5 all-gather.17
  424.0 153.7 all-reduce.5
where the time goes:
time: 594 us; the launch traced here: 588 us
  local copies, waits for them, and re-layouts  199 us (34%)
  waiting for transfers between devices  168 us (28%)
  other arithmetic  62.2 us (10%)
  blocking collectives  61.8 us (10%)
  matrix products  54.1 us (9%)
  starting transfers between devices  26.4 us (4%)
  between operations  14.8 us (2%)
    gather x192, local copies, waits for them, and re-layouts  128 us
    psum x1, waiting for transfers between devices, per_device(): lax.psum((down_local, device_raising_matrix, device_fading_floor, device_...  93.5 us
    psum x1, blocking collectives, per_device(): lax.psum((down_local, device_raising_matrix, device_fading_floor, device_...  61.8 us
    all_gather x2, waiting for transfers between devices, gathered_total(): return lax.all_gather(array, axis).sum(0)  59.7 us
    while x8, other arithmetic  22.7 us
    dot_general x4, matrix products, sensitivity_each_segment(): jnp.einsum('tshi,thi,shi->tsh', decays, gate_matrix, lookup_matrix, preci...  17.9 us
  transfers between devices with their start and end apart: 10, of which 5 were waited for; matrix products, arithmetic and copies ran while one was open for 48% of the time, Pallas kernels for 0%

commit v1 on v0

v1 whole, which is shorter than its diff:
```python
from functools import partial

import jax
import jax.numpy as jnp
from jax import lax
from jax.experimental import pallas as pl
from jax.experimental.pallas import tpu as pltpu
from jax.sharding import PartitionSpec as P

F32 = jnp.float32
BF16 = jnp.bfloat16
MESH = pl.DeviceIdType.MESH
N_HEAD = 16
N_SEQ = 32
TOK = 128
COL = 256
HS = 64
RANK = 128
VMEM = pl.BlockSpec(memory_space=pltpu.VMEM)

ROWS_LANES = (((1,), (0,)), ((), ()))
LANES_LANES = (((1,), (1,)), ((), ()))


def mm(a, b, dims=ROWS_LANES):
    return lax.dot_general(a, b, dims, preferred_element_type=F32)


def parts(a, count):
    out = []
    for _ in range(count - 1):
        top = a.astype(BF16)
        out.append(top)
        a = a - top.astype(F32)
    out.append(a.astype(BF16))
    return out


def mm3(a, b, dims=ROWS_LANES):
    ah, al = parts(a, 2)
    bh, bl = parts(b, 2)
    return mm(ah, bh, dims) + (mm(ah, bl, dims) + mm(al, bh, dims))


def mm_right_exact(a, b, dims=ROWS_LANES, count=2):
    out = None
    for piece in parts(a, count):
        term = mm(piece, b, dims)
        out = term if out is None else out + term
    return out


def mm_left_exact(a, b, dims=ROWS_LANES, count=2):
    out = None
    for piece in parts(b, count):
        term = mm(a, piece, dims)
        out = term if out is None else out + term
    return out


def iota(shape, dim):
    return lax.broadcasted_iota(jnp.int32, shape, dim)


def head_of(index):
    return index // HS


def lower_ones(strict):
    row, col = iota((TOK, TOK), 0), iota((TOK, TOK), 1)
    keep = row > col if strict else row >= col
    return jnp.where(keep, 1.0, 0.0).astype(BF16)


def upper_ones():
    row, col = iota((TOK, TOK), 0), iota((TOK, TOK), 1)
    return jnp.where(row < col, 1.0, 0.0).astype(BF16)


def block_diagonal():
    return head_of(iota((COL, COL), 0)) == head_of(iota((COL, COL), 1))


def odd_rows():
    return (head_of(iota((COL, 128), 0)) % 2) == 1


def remote(src, dst, send_sem, recv_sem, to):
    return pltpu.make_async_remote_copy(
        src_ref=src, dst_ref=dst, send_sem=send_sem, recv_sem=recv_sem,
        device_id=to, device_id_type=MESH,
    )


def greet(barrier, to):
    pl.semaphore_signal(barrier, inc=1, device_id=to, device_id_type=MESH)


def comm_params(ident):
    return pltpu.CompilerParams(collective_id=ident, has_side_effects=True)


def loop(start, stop, body):
    def step(i, carry):
        body(i)
        return carry

    lax.fori_loop(start, stop, step, 0)


def head_total(me, part, land, full, sems):
    send1, recv1, send2, recv2 = sems

    def first(d):
        to = (me + d) % N_HEAD
        return remote(part.at[to], land.at[me], send1.at[to], recv1.at[me], {"head": to})

    def first_in(d):
        frm = (me + d) % N_HEAD
        return remote(part.at[frm], land.at[frm], send1.at[frm], recv1.at[frm], {"head": frm})

    def second(d):
        to = (me + d) % N_HEAD
        return remote(full.at[me], full.at[me], send2.at[to], recv2.at[me], {"head": to})

    def second_in(d):
        frm = (me + d) % N_HEAD
        return remote(full.at[frm], full.at[frm], send2.at[frm], recv2.at[frm], {"head": frm})

    loop(1, N_HEAD, lambda d: first(d).start())
    land[me] = part[me]
    loop(1, N_HEAD, lambda d: first_in(d).wait_recv())
    total = land[0]
    for j in range(1, N_HEAD):
        total = total + land[j]
    full[me] = total
    loop(1, N_HEAD, lambda d: second(d).start())

    def finish():
        loop(1, N_HEAD, lambda d: second_in(d).wait_recv())
        loop(1, N_HEAD, lambda d: first_in(d).wait_send())
        loop(1, N_HEAD, lambda d: second_in(d).wait_send())

    return finish


HEAD_SCRATCH = [
    pltpu.VMEM((N_HEAD, 8, 128), F32),
    pltpu.VMEM((N_HEAD, 8, 128), F32),
    pltpu.VMEM((N_HEAD, 8, 128), F32),
    pltpu.SemaphoreType.DMA((N_HEAD,)),
    pltpu.SemaphoreType.DMA((N_HEAD,)),
    pltpu.SemaphoreType.DMA((N_HEAD,)),
    pltpu.SemaphoreType.DMA((N_HEAD,)),
]


def shift_mix(x, carried, mix):
    previous = pltpu.roll(x, 1, 0)
    previous = jnp.where(iota((TOK, COL), 0) == 0, carried, previous)
    return x + mix * (previous - x)


def adapter_in_kernel(
    x_ref, mix_ref, down_ref, pre_ref, row_ref,
    tail, part, land, full, send1, recv1, send2, recv2, row_send, row_recv,
):
    h, s = lax.axis_index("head"), lax.axis_index("seq")
    after, ahead = (s + 1) % N_SEQ, (s + N_SEQ - 1) % N_SEQ
    barrier = pltpu.get_barrier_semaphore()
    loop(1, N_HEAD, lambda d: greet(barrier, {"head": (h + d) % N_HEAD}))
    greet(barrier, {"seq": after})
    greet(barrier, {"seq": ahead})
    pl.semaphore_wait(barrier, N_HEAD + 1)
    copy = remote(x_ref.at[pl.ds(TOK - 16, 16)], tail, row_send, row_recv, {"seq": after})
    copy.start()
    x = x_ref[...].astype(F32)
    mix = mix_ref[...]
    copy.wait()
    carried = jnp.where(s == 0, 0.0, tail[...].astype(F32)[15:16])
    row_ref[...] = jnp.broadcast_to(carried, (8, COL))
    value = mm3(shift_mix(x, carried, mix), down_ref[...])
    part[...] = value.reshape(N_HEAD, 8, 128)
    head_total(h, part, land, full, (send1, recv1, send2, recv2))()
    pre_ref[...] = full[...].reshape(TOK, RANK)


def adapter_in(x, mix, down):
    return pl.pallas_call(
        adapter_in_kernel,
        out_shape=(
            jax.ShapeDtypeStruct((TOK, RANK), F32),
            jax.ShapeDtypeStruct((8, COL), F32),
        ),
        in_specs=[VMEM] * 3,
        out_specs=(VMEM, VMEM),
        scratch_shapes=[pltpu.VMEM((16, COL), BF16), *HEAD_SCRATCH,
                        pltpu.SemaphoreType.DMA, pltpu.SemaphoreType.DMA],
        compiler_params=comm_params(0),
        cost_estimate=pl.CostEstimate(flops=10**10, bytes_accessed=10**5, transcendentals=0),
        name="adapter_in",
    )(x, mix, down)


def local_kernel(pre_ref, base_ref, up_ref, r_ref, k_ref, v_ref, dy_ref, mid_ref, w_ref, cum_ref, pack_ref):
    mid = jnp.tanh(pre_ref[...])
    mid_ref[...] = mid
    w = -jnp.exp(base_ref[...] + mm3(mid, up_ref[...]))
    w_ref[...] = w
    w_parts = parts(w, 3)
    ones = lower_ones(False)
    cumul = mm(ones, w_parts[0]) + (mm(ones, w_parts[1]) + mm(ones, w_parts[2]))
    cum_ref[...] = cumul
    before = cumul - w
    final = cumul[TOK - 1 : TOK]
    flat = jnp.ones((TOK, 128), BF16)
    w_t = [p.astype(F32).T.astype(BF16) for p in w_parts]
    total_rows = mm(w_t[0], flat) + (mm(w_t[1], flat) + mm(w_t[2], flat))
    to_end = jnp.exp(jnp.minimum(final - cumul, 0.0))
    own = block_diagonal()
    odd = odd_rows()

    def folded(left, right):
        wide = mm_right_exact(left.T, right)
        wide = jnp.where(own, wide, 0.0)
        return wide[:, :128] + wide[:, 128:]

    state = folded(k_ref[...].astype(F32) * to_end, v_ref[...])
    grad = folded(r_ref[...].astype(F32) * jnp.exp(before), dy_ref[...])
    packed = jnp.where(odd, pltpu.roll(state, 64, 1), state) + jnp.where(odd, grad, pltpu.roll(grad, 64, 1))
    pack_ref[:, 0] = packed.reshape(N_SEQ, 8, 128)
    pack_ref[:, 1] = jnp.exp(total_rows).reshape(N_SEQ, 8, 128)


def local_terms(pre, base, up, r, k, v, dy):
    wide = jax.ShapeDtypeStruct((TOK, COL), F32)
    return pl.pallas_call(
        local_kernel,
        out_shape=(jax.ShapeDtypeStruct((TOK, RANK), F32), wide, wide,
                   jax.ShapeDtypeStruct((N_SEQ, 2, 8, 128), F32)),
        in_specs=[VMEM] * 7,
        out_specs=(VMEM,) * 4,
        cost_estimate=pl.CostEstimate(flops=10**10, bytes_accessed=10**6, transcendentals=0),
        name="local_terms",
    )(pre, base, up, r, k, v, dy)


def state_kernel(pack_ref, out_ref, land, back, got, send1, recv1, send2, recv2):
    s = lax.axis_index("seq")
    barrier = pltpu.get_barrier_semaphore()
    loop(1, N_SEQ, lambda d: greet(barrier, {"seq": (s + d) % N_SEQ}))
    pl.semaphore_wait(barrier, N_SEQ - 1)

    def first(d):
        to = (s + d) % N_SEQ
        return remote(pack_ref.at[to], land.at[s], send1.at[to], recv1.at[s], {"seq": to})

    def first_in(d):
        frm = (s + d) % N_SEQ
        return remote(pack_ref.at[frm], land.at[frm], send1.at[frm], recv1.at[frm], {"seq": frm})

    def second(d):
        to = (s + d) % N_SEQ
        return remote(back.at[to], got.at[s], send2.at[to], recv2.at[s], {"seq": to})

    def second_in(d):
        frm = (s + d) % N_SEQ
        return remote(back.at[frm], got.at[frm], send2.at[frm], recv2.at[frm], {"seq": frm})

    loop(1, N_SEQ, lambda d: first(d).start())
    land[s] = pack_ref[s]
    loop(1, N_SEQ, lambda d: first_in(d).wait_recv())
    onward = jnp.zeros((8, 128), F32)
    forward = []
    for n in range(N_SEQ):
        forward.append(onward)
        onward = land[n, 1] * onward + land[n, 0]
    left = iota((8, 128), 1) < 64
    reverse = jnp.zeros((8, 128), F32)
    for n in reversed(range(N_SEQ)):
        back[n] = jnp.where(left, forward[n], reverse)
        reverse = land[n, 1] * reverse + land[n, 0]
    loop(1, N_SEQ, lambda d: second(d).start())
    got[s] = back[s]
    loop(1, N_SEQ, lambda d: second_in(d).wait_recv())
    out_ref[...] = got[...].reshape(COL, 128)
    loop(1, N_SEQ, lambda d: first_in(d).wait_send())
    loop(1, N_SEQ, lambda d: second_in(d).wait_send())


def state_exchange(pack):
    return pl.pallas_call(
        state_kernel,
        out_shape=jax.ShapeDtypeStruct((COL, 128), F32),
        in_specs=[VMEM],
        out_specs=VMEM,
        scratch_shapes=[
            pltpu.VMEM((N_SEQ, 2, 8, 128), F32),
            pltpu.VMEM((N_SEQ, 8, 128), F32),
            pltpu.VMEM((N_SEQ, 8, 128), F32),
            *[pltpu.SemaphoreType.DMA((N_SEQ,))] * 4,
        ],
        compiler_params=comm_params(1),
        cost_estimate=pl.CostEstimate(flops=10**10, bytes_accessed=10**5, transcendentals=0),
        name="state_exchange",
    )(pack)


def lane_cat(stacked):
    return jnp.concatenate([stacked[h * TOK : (h + 1) * TOK] for h in range(4)], axis=1)


def wkv_kernel(
    w_ref, cum_ref, state_ref, r_ref, k_ref, v_ref, dy_ref, u_ref, mid_ref, up_ref,
    proj_ref, part_ref, raise_ref, sums_ref,
):
    w, cumul = w_ref[...], cum_ref[...]
    before = cumul - w
    final = cumul[TOK - 1 : TOK]
    rb, kb, vb, dyb = r_ref[...], k_ref[...], v_ref[...], dy_ref[...]
    r, k, v, dy = (a.astype(F32) for a in (rb, kb, vb, dyb))
    u = u_ref[...]
    own = block_diagonal()
    odd = odd_rows()
    left = iota((COL, 128), 1) < 64
    packed = state_ref[...]
    state = jnp.where(left, packed, 0.0)
    grad = jnp.where(left, 0.0, packed)
    state = jnp.where(odd, pltpu.roll(state, 64, 1), state)
    grad = jnp.where(odd, grad, pltpu.roll(grad, 64, 1))
    state = jnp.where(own, jnp.concatenate([state, state], axis=1), 0.0)
    grad = jnp.where(own, jnp.concatenate([grad, grad], axis=1), 0.0)

    to_end = jnp.exp(jnp.minimum(final - cumul, 0.0))
    gr_mem = jnp.exp(before) * mm_left_exact(dyb, state, LANES_LANES)
    gk_out = to_end * mm_left_exact(vb, grad, LANES_LANES)
    gv = mm3(k * to_end, grad)
    across = mm_left_exact(jnp.ones((8, COL), BF16), state * grad, LANES_LANES, 3)[0:1] * jnp.exp(final)

    lane_head = head_of(iota((TOK, COL), 1))
    heads = [lane_head == h for h in range(4)]
    zero16 = jnp.zeros((TOK, COL), BF16)

    def by_head(a):
        return jnp.concatenate([jnp.where(m, a, zero16) for m in heads], axis=0)

    v_heads, dy_heads = by_head(vb), by_head(dyb)
    pair_ts = mm(dy_heads, vb, LANES_LANES)
    pair_st = mm(v_heads, dyb, LANES_LANES)
    ts_top, ts_low = (lane_cat(p) for p in parts(pair_ts, 2))
    st_top, st_low = (lane_cat(p) for p in parts(pair_st, 2))

    def wide_mm(top, low, mask, factor):
        f_top, f_low = (by_head(p) for p in parts(factor, 2))
        zero = jnp.zeros((TOK, 4 * TOK), BF16)
        top, low = jnp.where(mask, top, zero), jnp.where(mask, low, zero)
        return mm(top, f_top) + (mm(top, f_low) + mm(low, f_top))

    gk_in = jnp.zeros((TOK, COL), F32)
    score_st = jnp.zeros((4 * TOK, TOK), F32)
    tok = iota((TOK, COL), 0)
    for half in (64, 32, 16, 8):
        size = 2 * half
        second = (tok % size) >= half
        middle = cumul.reshape(TOK // size, size, COL)[:, half - 1 : half]
        middle = jnp.broadcast_to(middle, (TOK // size, size, COL)).reshape(TOK, COL)
        fade = jnp.exp(jnp.minimum(jnp.where(second, before - middle, middle - cumul), 0.0))
        late, early = jnp.where(second, fade, 0.0), jnp.where(second, 0.0, fade)
        r_hat, k_hat = r * late, k * early
        block_row = iota((TOK, 4 * TOK), 0) // size
        block_col = (iota((TOK, 4 * TOK), 1) % TOK) // size
        same = block_row == block_col
        gr_mem = gr_mem + late * wide_mm(ts_top, ts_low, same, k_hat)
        gk_in = gk_in + early * wide_mm(st_top, st_low, same, r_hat)
        k_top, k_low = (by_head(p) for p in parts(k_hat, 2))
        r_top, r_low = parts(r_hat, 2)
        score = mm(k_top, r_top, LANES_LANES) + (mm(k_top, r_low, LANES_LANES) + mm(k_low, r_top, LANES_LANES))
        same_st = ((iota((4 * TOK, TOK), 0) % TOK) // size) == (iota((4 * TOK, TOK), 1) // size)
        score_st = score_st + jnp.where(same_st, score, 0.0)
    for piece in parts(score_st, 2):
        gv = gv + mm(lane_cat(piece), dy_heads)

    spread = jnp.where(own, 1.0, 0.0).astype(BF16)

    def tiles(a):
        return a.reshape(TOK // 8, 8, COL)

    def flat(a):
        return a.reshape(TOK, COL)

    sub = iota((TOK // 8, 8, COL), 1)
    for d in range(1, 8):
        valid = sub >= d
        cum_old = pltpu.roll(tiles(cumul), d, 1)
        k_old = pltpu.roll(tiles(k), d, 1)
        v_old = pltpu.roll(tiles(v), d, 1)
        fade = jnp.exp(jnp.minimum(jnp.where(valid, tiles(before) - cum_old, 0.0), 0.0))
        fade = flat(jnp.where(valid, fade, 0.0))
        pair = mm_right_exact(dy * flat(v_old), spread)
        faded_r = fade * r
        gr_mem = gr_mem + fade * pair * flat(k_old)
        gk_in = gk_in + flat(pltpu.roll(tiles(faded_r * pair), 8 - d, 1))
        score = mm_right_exact(faded_r * flat(k_old), spread)
        gv = gv + flat(pltpu.roll(tiles(score * dy), 8 - d, 1))

    self_pair = mm_right_exact(dy * v, spread)
    self_score = mm_right_exact(r * u * k, spread)
    gv = gv + self_score * dy
    r_pair = r * self_pair
    proj_ref[0] = (gr_mem + u * k * self_pair).astype(BF16)
    proj_ref[1] = (gk_in + gk_out + u * r_pair).astype(BF16)
    proj_ref[2] = gv.astype(BF16)

    k_in = k * gk_in
    g_log = across - k_in + mm_left_exact(lower_ones(True), k * gk_out)
    g_log = g_log + mm_left_exact(upper_ones(), r * gr_mem - k_in)
    g_pre = g_log * w
    part_ref[...] = mm3(g_pre, up_ref[...], LANES_LANES).reshape(N_HEAD, 8, 128)
    raise_ref[...] = mm3(mid_ref[...].T, g_pre)
    floor_row = jnp.sum(g_pre, axis=0, keepdims=True)
    bonus_row = jnp.sum(k * r_pair, axis=0, keepdims=True)
    row = iota((8, COL), 0)
    sums_ref[...] = jnp.where(row == 0, floor_row, jnp.where(row == 1, bonus_row, 0.0))


def wkv_grads(w, cumul, state, r, k, v, dy, u, mid, up):
    return pl.pallas_call(
        wkv_kernel,
        out_shape=(
            jax.ShapeDtypeStruct((3, TOK, COL), BF16),
            jax.ShapeDtypeStruct((N_HEAD, 8, 128), F32),
            jax.ShapeDtypeStruct((RANK, COL), F32),
            jax.ShapeDtypeStruct((8, COL), F32),
        ),
        in_specs=[VMEM] * 10,
        out_specs=(VMEM,) * 4,
        cost_estimate=pl.CostEstimate(flops=10**10, bytes_accessed=10**6, transcendentals=0),
        name="wkv_grads",
    )(w, cumul, state, r, k, v, dy, u, mid, up)


def adapter_out_kernel(
    part_ref, proj_ref, mid_out, both_ref,
    land, full, send1, recv1, send2, recv2, swap_send, swap_recv, near_send, near_recv, edge_in, far_send, far_recv,
):
    h, s = lax.axis_index("head"), lax.axis_index("seq")
    core = h % 2
    mate = h + 1 - 2 * core
    after, ahead = (s + 1) % N_SEQ, (s + N_SEQ - 1) % N_SEQ
    barrier = pltpu.get_barrier_semaphore()
    loop(1, N_HEAD, lambda d: greet(barrier, {"head": (h + d) % N_HEAD}))
    for other in (after, ahead):
        greet(barrier, {"seq": other})
        greet(barrier, {"seq": other, "head": mate})
    pl.semaphore_wait(barrier, N_HEAD + 3)
    swap = remote(proj_ref, both_ref.at[core, :, pl.ds(0, TOK)], swap_send, swap_recv, {"head": mate})
    swap.start()
    edge = proj_ref.at[:, pl.ds(0, 16)]
    near = remote(edge, edge_in.at[core], near_send, near_recv, {"seq": ahead})
    far = remote(edge, edge_in.at[core], far_send, far_recv, {"seq": ahead, "head": mate})
    near.start()
    far.start()
    both_ref[core, :, pl.ds(0, TOK)] = proj_ref[...]
    finish = head_total(h, part_ref, land, full, (send1, recv1, send2, recv2))
    near.wait()
    far.wait()
    last = s == N_SEQ - 1
    both_ref[:, :, pl.ds(TOK, 16)] = jnp.where(last, jnp.zeros((2, 3, 16, COL), BF16), edge_in[...])
    finish()
    mid_out[...] = full[...].reshape(TOK, RANK)
    swap.wait()


def adapter_out(part, proj):
    return pl.pallas_call(
        adapter_out_kernel,
        out_shape=(
            jax.ShapeDtypeStruct((TOK, RANK), F32),
            jax.ShapeDtypeStruct((2, 3, TOK + 16, COL), BF16),
        ),
        in_specs=[VMEM] * 2,
        out_specs=(VMEM, VMEM),
        scratch_shapes=[
            *HEAD_SCRATCH[1:],
            *[pltpu.SemaphoreType.DMA] * 4,
            pltpu.VMEM((2, 3, 16, COL), BF16),
            *[pltpu.SemaphoreType.DMA] * 2,
        ],
        compiler_params=comm_params(2),
        cost_estimate=pl.CostEstimate(flops=10**10, bytes_accessed=10**6, transcendentals=0),
        name="adapter_out",
    )(part, proj)


def adapter_grads_kernel(raw_ref, mid_ref, x_ref, row_ref, mix_ref, down_ref, raise_ref, sums_ref, gdi_ref, big_ref):
    mid = mid_ref[...]
    g_mid = raw_ref[...] * (1.0 - mid * mid)
    down_t = down_ref[...]
    gdi_ref[...] = mm3(g_mid, down_t, LANES_LANES)
    decay_in = shift_mix(x_ref[...].astype(F32), row_ref[0:1], mix_ref[...])
    big_ref[0:16, 0:16] = mm3(decay_in.T, g_mid).reshape(16, 16, 128)
    big_ref[16:24, 0:16] = raise_ref[:, 0:128].reshape(8, 16, 128)
    big_ref[24:32, 0:16] = raise_ref[:, 128:256].reshape(8, 16, 128)
    sums = sums_ref[...]
    small = jnp.where(iota((8, 128), 0) < 2, sums[:, 0:128], pltpu.roll(sums[:, 128:256], 2, 0))
    big_ref[:, 16:24] = jnp.broadcast_to(small[None], (N_SEQ, 8, 128))


def adapter_grads(raw, mid, x, row, mix, down, raising, sums):
    return pl.pallas_call(
        adapter_grads_kernel,
        out_shape=(
            jax.ShapeDtypeStruct((TOK, COL), F32),
            jax.ShapeDtypeStruct((N_SEQ, 24, 128), F32),
        ),
        in_specs=[VMEM] * 8,
        out_specs=(VMEM, VMEM),
        cost_estimate=pl.CostEstimate(flops=10**9, bytes_accessed=10**6, transcendentals=0),
        name="adapter_grads",
    )(raw, mid, x, row, mix, down, raising, sums)


def project_kernel(both_ref, w_ref, mix_ref, out_ref):
    own = jnp.zeros((TOK, 128), F32)
    prior = jnp.zeros((TOK + 16, 128), F32)
    mixes = mix_ref[0]
    for m in range(3):
        weights = w_ref[:, m].reshape(128, 2 * COL)
        term = mm(both_ref[0, m], weights[:, :COL], LANES_LANES) + mm(both_ref[1, m], weights[:, COL:], LANES_LANES)
        mix = mixes[m : m + 1]
        own = own + (1.0 - mix) * term[:TOK]
        prior = prior + mix * term
    out_ref[0] = (own + pltpu.roll(prior, TOK + 15, 0)[:TOK]).astype(BF16)


def project(both, weights, mixes):
    return pl.pallas_call(
        project_kernel,
        grid=(N_HEAD,),
        out_shape=jax.ShapeDtypeStruct((N_HEAD, TOK, 128), BF16),
        in_specs=[
            pl.BlockSpec((2, 3, TOK + 16, COL), lambda i: (0, 0, 0, 0)),
            pl.BlockSpec((2, 3, 64, 2 * COL), lambda i: (i, 0, 0, 0)),
            pl.BlockSpec((1, 8, 128), lambda i: (i, 0, 0)),
        ],
        out_specs=pl.BlockSpec((1, TOK, 128), lambda i: (i, 0, 0)),
        cost_estimate=pl.CostEstimate(flops=10**10, bytes_accessed=10**7, transcendentals=0),
        name="project",
    )(both, weights, mixes)


def last_kernel(
    y_ref, big_ref, gdi_ref, mix_ref, out_ref, down_ref, raise_ref, small_ref,
    y_in, big_in, total, edge, y_send, y_recv, send1, recv1, send2, recv2, e_send, e_recv,
):
    h, s = lax.axis_index("head"), lax.axis_index("seq")
    after, ahead = (s + 1) % N_SEQ, (s + N_SEQ - 1) % N_SEQ
    barrier = pltpu.get_barrier_semaphore()
    loop(1, N_HEAD, lambda d: greet(barrier, {"head": (h + d) % N_HEAD}))
    loop(1, N_SEQ, lambda d: greet(barrier, {"seq": (s + d) % N_SEQ}))
    pl.semaphore_wait(barrier, N_HEAD + N_SEQ - 2)

    def y_out(d):
        to = (h + d) % N_HEAD
        return remote(y_ref.at[to], y_in.at[h], y_send.at[to], y_recv.at[h], {"head": to})

    def y_from(d):
        frm = (h + d) % N_HEAD
        return remote(y_ref.at[frm], y_in.at[frm], y_send.at[frm], y_recv.at[frm], {"head": frm})

    def first(d):
        to = (s + d) % N_SEQ
        return remote(big_ref.at[to], big_in.at[s], send1.at[to], recv1.at[s], {"seq": to})

    def first_in(d):
        frm = (s + d) % N_SEQ
        return remote(big_ref.at[frm], big_in.at[frm], send1.at[frm], recv1.at[frm], {"seq": frm})

    def second(d):
        to = (s + d) % N_SEQ
        return remote(total.at[s], total.at[s], send2.at[to], recv2.at[s], {"seq": to})

    def second_in(d):
        frm = (s + d) % N_SEQ
        return remote(total.at[frm], total.at[frm], send2.at[frm], recv2.at[frm], {"seq": frm})

    loop(1, N_SEQ, lambda d: first(d).start())
    loop(1, N_HEAD, lambda d: y_out(d).start())
    row_copy = remote(gdi_ref.at[pl.ds(0, 8)], edge, e_send, e_recv, {"seq": ahead})
    row_copy.start()
    big_in[s] = big_ref[s]
    y_in[h] = y_ref[h]
    loop(1, N_SEQ, lambda d: first_in(d).wait_recv())
    acc = big_in[0]
    for n in range(1, N_SEQ):
        acc = acc + big_in[n]
    total[s] = acc[:16]
    loop(1, N_SEQ, lambda d: second(d).start())
    small_ref[...] = acc[16:24]
    row_copy.wait()
    gdi = gdi_ref[...]
    next_row = jnp.where(s == N_SEQ - 1, 0.0, edge[0:1])
    shifted = jnp.where(iota((TOK, COL), 0) == TOK - 1, next_row, pltpu.roll(gdi, TOK - 1, 0))
    mix = mix_ref[...]
    mine = (1.0 - mix) * gdi + mix * shifted
    loop(1, N_HEAD, lambda d: y_from(d).wait_recv())
    halves = []
    for core in range(2):
        acc = y_in[core].astype(F32)
        for y in range(1, 8):
            acc = acc + y_in[2 * y + core].astype(F32)
        halves.append(acc)
    low = iota((TOK, 128), 1) < 64
    even = jnp.where(low, halves[0], pltpu.roll(halves[1], 64, 1))
    odd = jnp.where(low, pltpu.roll(halves[0], 64, 1), halves[1])
    out_ref[:, 0:128] = (even + mine[:, 0:128]).astype(BF16)
    out_ref[:, 128:256] = (odd + mine[:, 128:256]).astype(BF16)
    loop(1, N_SEQ, lambda d: second_in(d).wait_recv())
    down_ref[...] = total[0:16].reshape(COL, RANK)
    raise_ref[:, 0:128] = total[16:24].reshape(RANK, 128)
    raise_ref[:, 128:256] = total[24:32].reshape(RANK, 128)
    loop(1, N_HEAD, lambda d: y_from(d).wait_send())
    loop(1, N_SEQ, lambda d: first_in(d).wait_send())
    loop(1, N_SEQ, lambda d: second_in(d).wait_send())


def last(y, big, gdi, mix):
    return pl.pallas_call(
        last_kernel,
        out_shape=(
            jax.ShapeDtypeStruct((TOK, COL), BF16),
            jax.ShapeDtypeStruct((COL, RANK), F32),
            jax.ShapeDtypeStruct((RANK, COL), F32),
            jax.ShapeDtypeStruct((8, 128), F32),
        ),
        in_specs=[VMEM] * 4,
        out_specs=(VMEM,) * 4,
        scratch_shapes=[
            pltpu.VMEM((N_HEAD, TOK, 128), BF16),
            pltpu.VMEM((N_SEQ, 24, 128), F32),
            pltpu.VMEM((N_SEQ, 16, 128), F32),
            pltpu.VMEM((8, COL), F32),
            *[pltpu.SemaphoreType.DMA((N_HEAD,))] * 2,
            *[pltpu.SemaphoreType.DMA((N_SEQ,))] * 4,
            *[pltpu.SemaphoreType.DMA] * 2,
        ],
        compiler_params=comm_params(3),
        cost_estimate=pl.CostEstimate(flops=10**10, bytes_accessed=10**6, transcendentals=0),
        name="last",
    )(y, big, gdi, mix)


def gathered_weights(proj_weights):
    head = lax.axis_index("head")
    core = head % 2
    keep = lax.dynamic_slice_in_dim(proj_weights, core * 64, 64, 1)
    give = lax.dynamic_slice_in_dim(proj_weights, (1 - core) * 64, 64, 1)
    taken = lax.ppermute(give, "head", [(i, i ^ 1) for i in range(N_HEAD)])
    first = core == 0
    mine = jnp.concatenate([jnp.where(first, keep, taken), jnp.where(first, taken, keep)], axis=2)
    return lax.all_gather(mine, "seq")


def per_device(
    layer_input, receptance, key_act, value_act, attention_result_sensitivity, time_first,
    decay_exponent_base, decay_shift_mix, mix_rkv, decay_adapter_down, decay_adapter_up, proj_weights,
):
    weights = gathered_weights(proj_weights)
    core = lax.axis_index("head") % 2
    mixes = lax.dynamic_index_in_dim(mix_rkv.reshape(3, N_HEAD, 2, 2, 64), core, 3, keepdims=False)
    mixes = jnp.moveaxis(mixes.reshape(3, N_HEAD, 128), 0, 1)
    mixes = jnp.pad(mixes, ((0, 0), (0, 5), (0, 0)))
    mix = decay_shift_mix[None]
    u = time_first.reshape(1, COL)
    acts = (receptance, key_act, value_act, attention_result_sensitivity)
    pre, row = adapter_in(layer_input, mix, decay_adapter_down)
    mid, w, cumul, pack = local_terms(pre, decay_exponent_base[None], decay_adapter_up, *acts)
    state = state_exchange(pack)
    proj, part, raising, sums = wkv_grads(w, cumul, state, *acts, u, mid, decay_adapter_up)
    raw, both = adapter_out(part, proj)
    gdi, big = adapter_grads(raw, mid, layer_input, row, mix, decay_adapter_down, raising, sums)
    y = project(both, weights, mixes)
    out, down_grad, up_grad, small = last(y, big, gdi, mix)
    base_grad = jnp.concatenate([small[0], small[2]])
    bonus_grad = jnp.concatenate([small[1], small[3]]).reshape(4, HS)
    return out, down_grad, up_grad, base_grad, bonus_grad


def solution(mesh):
    return jax.shard_map(
        per_device,
        mesh=mesh,
        in_specs=(
            P("seq", "head"), P("seq", "head"), P("seq", "head"), P("seq", "head"), P("seq", "head"),
            P("head", None), P("head"), P("head"), P(), P("head", None), P(None, "head"),
            P(None, "seq", "head"),
        ),
        out_specs=(P("seq", "head"), P("head", None), P(None, "head"), P("head"), P("head", None)),
        check_vma=False,
    )
```

time: 594 us -> 171 us (0.29)
  local copies, waits for them, and re-layouts: 199 us -> 9.61 us
  waiting for transfers between devices: 168 us -> 16.2 us
  Pallas kernels: 0 us -> 125 us
  blocking collectives: 61.8 us -> 0 us
  other arithmetic: 62.2 us -> 2.79 us
  matrix products: 54.1 us -> 0 us
  starting transfers between devices: 26.4 us -> 1.95 us
    gather x194 -> x0, local copies, waits for them, and re-layouts: 129 us -> none
    pallas_call x0 -> x8, Pallas kernels: none -> 125 us  [the longest x1 32 us: last(): pl.pallas_call(last_kernel, out_shape=(jax.ShapeDtypeStruct((TOK, COL), B...]
    psum x1 -> x0, waiting for transfers between devices: 93.5 us -> none  [per_device(): lax.psum((down_local, device_raising_matrix, device_fading_floor, device_...]
    psum x1 -> x0, blocking collectives: 61.8 us -> none  [per_device(): lax.psum((down_local, device_raising_matrix, device_fading_floor, device_...]
    dot_general x44 -> x0, matrix products: 54.1 us -> none  [the longest x4 17.9 us: sensitivity_each_segment(): jnp.einsum('tshi,thi,shi->tsh', decays, gate_matrix, lookup_matrix, preci...]
    all_gather x5 -> x1, waiting for transfers between devices: 59.7 us -> 15 us  [gathered_weights(): return lax.all_gather(mine, 'seq')]
    while x8 -> x0, other arithmetic: 22.7 us -> none
    all_to_all x2 -> x0, starting transfers between devices: 15.3 us -> none  [the longest x1 10.5 us: sent_to_all(): return lax.all_to_all(copies, axis, split_axis=0, concat_axis=0, tiled=True)]
  transfers between devices with their start and end apart: 10 -> 2, of which waited for: 5 -> 2; matrix products, arithmetic and copies ran while one was open for 48% -> 2% of each run, Pallas kernels for 0% -> 48%
where the time goes in v1:
time: 171 us; the launch traced here: 170 us
  Pallas kernels  125 us (73%)
  waiting for transfers between devices  16.2 us (9%)
  between operations  14.1 us (8%)
  local copies, waits for them, and re-layouts  9.61 us (6%)
  other arithmetic  2.79 us (2%)
  starting transfers between devices  1.95 us (1%)
    pallas_call x1, Pallas kernels, last(): pl.pallas_call(last_kernel, out_shape=(jax.ShapeDtypeStruct((TOK, COL), B...  32 us
    pallas_call x1, Pallas kernels, adapter_in(): pl.pallas_call(adapter_in_kernel, out_shape=(jax.ShapeDtypeStruct((TOK, R...  30.4 us
    pallas_call x1, Pallas kernels, state_exchange(): pl.pallas_call(state_kernel, out_shape=jax.ShapeDtypeStruct((COL, 128), F...  24.5 us
    pallas_call x1, Pallas kernels, adapter_out(): pl.pallas_call(adapter_out_kernel, out_shape=(jax.ShapeDtypeStruct((TOK,...  16.1 us
    all_gather x1, waiting for transfers between devices, gathered_weights(): return lax.all_gather(mine, 'seq')  15 us
    pallas_call x1, Pallas kernels, project(): pl.pallas_call(project_kernel, grid=(N_HEAD,), out_shape=jax.ShapeDtypeSt...  12 us
    pallas_call x1, Pallas kernels, wkv_grads(): pl.pallas_call(wkv_kernel, out_shape=(jax.ShapeDtypeStruct((3, TOK, COL),...  5.73 us
    unnamed x3, local copies, waits for them, and re-layouts  4.61 us
  transfers between devices with their start and end apart: 2, of which 2 were waited for; matrix products, arithmetic and copies ran while one was open for 2% of the time, Pallas kernels for 48%

profile of v1, /device:TPU:6, one launch (start us, length us, event | category | flops | bytes accessed | tf_op | source)
XLA Modules:
  0.0 170.2 jit_solution(4858817799458894775)
XLA Ops:
  7.2 0.0 all-gather.3.cloned.1.call-start
  7.2 0.9 constant_dynamic-slice_fusion.1
  8.1 1.9 %collective-permute-start = (bf16[3,64,256]{2,1,0:T(8,128)(2,1)S(1)}, bf16[3,64,256]{2,1,0:T(8,128)(2,1)S(1)}, u32[]{:S(2)}, u32[]{:S(2)}) collective-permute-start(bf16[3,64,256]{2,1,0:T(8,128)(2,1)S(1)} %constant_dynamic-slice_fusion.1), channel_id=1, source_target_pairs={{0,32},{32,0},{64,96},{96,64},{128,160},{160,128},{192,224},{224,1... | collective-permute-start | bytes 294920 | tf_op jit(solution)/shard_map/ppermute | solution.py:658
  10.1 1.3 collective-permute-done
  11.3 0.9 broadcast_select_fusion.1
  12.3 0.7 pad_maximum_fusion
  13.0 0.0 all-gather.3.cloned.1.call-update
  13.0 1.3 reshape.25.u_ref
  14.3 1.0 reshape.26
  15.3 0.1 reshape.27
  15.5 0.6 pad.4.mix_ref
  16.1 30.4 %adapter_in.1 = (f32[128,128]{1,0:T(8,128)}, f32[8,256]{1,0:T(8,128)}) custom-call(bf16[128,256]{1,0:T(8,128)(2,1)} %x_ref.3, f32[1,256]{1,0:T(1,128)} %bitcast.17, f32[256,128]{1,0:T(8,128)} %down_ref.3), custom_call_target="tpu_custom_call" | custom-call | flops 10000000000 | bytes 100000 | tf_op jit(solution)/shard_map/adapter_in/pallas_call | solution.py:189
  46.5 2.7 %local_terms.1 = (f32[128,128]{1,0:T(8,128)}, f32[128,256]{1,0:T(8,128)}, f32[128,256]{1,0:T(8,128)}, f32[32,2,8,128]{3,2,1,0:T(8,128)}) custom-call(f32[128,128]{1,0:T(8,128)} %get-tuple-element.23.pre_ref, f32[1,256]{1,0:T(1,128)} %bitcast.16, f32[128,256]{1,0:T(8,128)} %up_ref.3, bf16[128,256]{1,0:T(8,128)(2,1)} %r_ref.3, bf16[128,256]{1,0:T(8,128)(2,1)} %k_ref.3, ...), custom_call_target="tpu_custom_call" | custom-call | flops 10000000000 | bytes 1000000 | tf_op jit(solution)/shard_map/local_terms/pallas_call | solution.py:237
  49.2 24.5 %state_exchange.1.state_ref = f32[256,128]{1,0:T(8,128)} custom-call(f32[32,2,8,128]{3,2,1,0:T(8,128)} %get-tuple-element.26.pack_ref), custom_call_target="tpu_custom_call" | custom-call | flops 10000000000 | bytes 100000 | tf_op jit(solution)/shard_map/state_exchange/pallas_call | solution.py:292
  73.6 5.7 %wkv_grads.1 = (bf16[3,128,256]{2,1,0:T(8,128)(2,1)}, f32[16,8,128]{2,1,0:T(8,128)}, f32[128,256]{1,0:T(8,128)}, f32[8,256]{1,0:T(8,128)}) custom-call(f32[128,256]{1,0:T(8,128)} %get-tuple-element.24.w_ref, f32[128,256]{1,0:T(8,128)} %get-tuple-element.25.cum_ref, f32[256,128]{1,0:T(8,128)} %state_exchange.1.state_ref, bf16[128,256]{1,0:T(8,128)(2,1)} %r_ref.3, ...), custom_call_target="tpu_custom_call" | custom-call | flops 10000000000 | bytes 1000000 | tf_op jit(solution)/shard_map/wkv_grads/pallas_call | solution.py:427
  79.4 16.1 %adapter_out.1 = (f32[128,128]{1,0:T(8,128)}, bf16[2,3,144,256]{3,2,1,0:T(8,128)(2,1)}) custom-call(f32[16,8,128]{2,1,0:T(8,128)} %get-tuple-element.28.part_ref, bf16[3,128,256]{2,1,0:T(8,128)(2,1)} %get-tuple-element.29.proj_ref), custom_call_target="tpu_custom_call" | custom-call | flops 10000000000 | bytes 1000000 | tf_op jit(solution)/shard_map/adapter_out/pallas_call | solution.py:475
  95.4 2.2 %adapter_grads.1 = (f32[128,256]{1,0:T(8,128)}, f32[32,24,128]{2,1,0:T(8,128)}) custom-call(f32[128,128]{1,0:T(8,128)} %get-tuple-element.31.raw_ref, f32[128,128]{1,0:T(8,128)} %get-tuple-element.27.mid_ref, bf16[128,256]{1,0:T(8,128)(2,1)} %x_ref.3, f32[8,256]{1,0:T(8,128)} %get-tuple-element.32.row_ref, f32[1,256]{1,0:T(1,128)} %bitcast.18, ...), custom_call_target="tpu_custom_call" | custom-call | flops 1000000000 | bytes 1000000 | tf_op jit(solution)/shard_map/adapter_grads/pallas_call | solution.py:510
  97.6 15.0 %all-gather.3.cloned.1.call-done = bf16[96,64,512]{2,1,0:T(8,128)(2,1)} async-done(((bf16[3,64,512]{2,1,0:T(8,128)(2,1)}), bf16[96,64,512]{2,1,0:T(8,128)(2,1)}) %all-gather.3.cloned.1.call-update) | async-done | bytes 6291472 | tf_op jit(solution)/shard_map/all_gather | solution.py:661
  112.6 12.0 %project.1.y_ref = bf16[16,128,128]{2,1,0:T(8,128)(2,1)} custom-call(bf16[2,3,144,256]{3,2,1,0:T(8,128)(2,1)} %get-tuple-element.30.both_ref, bf16[32,3,64,512]{3,2,1,0:T(8,128)(2,1)} %bitcast.15, f32[16,8,128]{2,1,0:T(8,128)} %pad.4.mix_ref), custom_call_target="tpu_custom_call" | custom-call | flops 10000000000 | bytes 10000000 | tf_op jit(solution)/shard_map/project/pallas_call | solution.py:537
  124.6 32.0 %last.1 = (bf16[128,256]{1,0:T(8,128)(2,1)}, f32[256,128]{1,0:T(8,128)}, f32[128,256]{1,0:T(8,128)}, f32[8,128]{1,0:T(8,128)}) custom-call(bf16[16,128,128]{2,1,0:T(8,128)(2,1)} %project.1.y_ref, f32[32,24,128]{2,1,0:T(8,128)} %get-tuple-element.35.big_ref, f32[128,256]{1,0:T(8,128)} %get-tuple-element.36.gdi_ref, f32[1,256]{1,0:T(1,128)} %bitcast.19), custom_call_target="tpu_custom_call" | custom-call | flops 10000000000 | bytes 1000000 | tf_op jit(solution)/shard_map/last/pallas_call | solution.py:628
  156.6 0.8 slice_reduce_fusion.1
  157.4 0.1 concatenate.16
  157.5 0.1 concatenate.17
  157.6 0.6 pad_maximum_fusion.1
  158.2 0.6 pad_maximum_fusion.2
  158.7 1.5 copy.28
  160.2 1.6 copy.29
  161.8 1.6 copy.30
  (2 shorter events, 0.1 us)
Async XLA Ops:
  7.2 105.4 %all-gather.3.cloned.1.call-start = ((), (), s32[]{:S(2)}) async-start(), calls=%async_computation | async-start | bytes 6488064 | tf_op jit(solution)/shard_map/all_gather | solution.py:661
  8.1 3.2 %collective-permute-start = (bf16[3,64,256]{2,1,0:T(8,128)(2,1)S(1)}, bf16[3,64,256]{2,1,0:T(8,128)(2,1)S(1)}, u32[]{:S(2)}, u32[]{:S(2)}) collective-permute-start(bf16[3,64,256]{2,1,0:T(8,128)(2,1)S(1)} %constant_dynamic-slice_fusion.1), channel_id=1, source_target_pairs={{0,32},{32,0},{64,96},{96,64},{128,160},{160,128},{192,224},{224,1... | collective-permute-start | bytes 294920 | tf_op jit(solution)/shard_map/ppermute | solution.py:658
Sparse Core Ops, SparseCore 0:
  13.1 99.4 all-gather.2

commit v2 on v0

v2 whole, which is shorter than its diff:
```python
from types import SimpleNamespace

import jax
import jax.numpy as jnp
from jax import lax
from jax.experimental import pallas as pl
from jax.experimental.pallas import tpu as pltpu
from jax.sharding import PartitionSpec as P

F32 = jnp.float32
BF16 = jnp.bfloat16
MESH = pl.DeviceIdType.MESH
N_HEAD = 16
N_SEQ = 32
TOK = 128
COL = 256
HS = 64
RANK = 128
VMEM = pl.BlockSpec(memory_space=pltpu.VMEM)

ROWS_LANES = (((1,), (0,)), ((), ()))
LANES_LANES = (((1,), (1,)), ((), ()))


def mm(a, b, dims=ROWS_LANES):
    return lax.dot_general(a, b, dims, preferred_element_type=F32)


def parts(a, count):
    out = []
    for _ in range(count - 1):
        top = a.astype(BF16)
        out.append(top)
        a = a - top.astype(F32)
    out.append(a.astype(BF16))
    return out


def mm3(a, b, dims=ROWS_LANES):
    ah, al = parts(a, 2)
    bh, bl = parts(b, 2)
    return mm(ah, bh, dims) + (mm(ah, bl, dims) + mm(al, bh, dims))


def mm_right_exact(a, b, dims=ROWS_LANES, count=2):
    out = None
    for piece in parts(a, count):
        term = mm(piece, b, dims)
        out = term if out is None else out + term
    return out


def mm_left_exact(a, b, dims=ROWS_LANES, count=2):
    out = None
    for piece in parts(b, count):
        term = mm(a, piece, dims)
        out = term if out is None else out + term
    return out


def iota(shape, dim):
    return lax.broadcasted_iota(jnp.int32, shape, dim)


def head_of(index):
    return index // HS


def lower_ones(strict):
    row, col = iota((TOK, TOK), 0), iota((TOK, TOK), 1)
    keep = row > col if strict else row >= col
    return jnp.where(keep, 1.0, 0.0).astype(BF16)


def upper_ones():
    row, col = iota((TOK, TOK), 0), iota((TOK, TOK), 1)
    return jnp.where(row < col, 1.0, 0.0).astype(BF16)


def block_diagonal():
    return head_of(iota((COL, COL), 0)) == head_of(iota((COL, COL), 1))


def odd_rows():
    return (head_of(iota((COL, 128), 0)) % 2) == 1


def remote(src, dst, send_sem, recv_sem, to):
    return pltpu.make_async_remote_copy(
        src_ref=src, dst_ref=dst, send_sem=send_sem, recv_sem=recv_sem,
        device_id=to, device_id_type=MESH,
    )


def greet(barrier, to):
    pl.semaphore_signal(barrier, inc=1, device_id=to, device_id_type=MESH)


def loop(start, stop, body):
    def step(i, carry):
        body(i)
        return carry

    lax.fori_loop(start, stop, step, 0)


def shift_mix(x, carried, mix):
    previous = pltpu.roll(x, 1, 0)
    previous = jnp.where(iota((TOK, COL), 0) == 0, carried, previous)
    return x + mix * (previous - x)


class AllToAll:
    def __init__(self, axis, size, me, out, land, send, recv, broadcast=False):
        self.axis, self.size, self.me = axis, size, me
        self.out, self.land, self.send, self.recv, self.broadcast = out, land, send, recv, broadcast

    def _to(self, peer):
        src = self.out.at[self.me if self.broadcast else peer]
        return remote(src, self.land.at[self.me], self.send.at[peer], self.recv.at[self.me], {self.axis: peer})

    def _from(self, peer):
        src = self.out.at[self.me if self.broadcast else peer]
        return remote(src, self.land.at[peer], self.send.at[peer], self.recv.at[peer], {self.axis: peer})

    def _each(self, act):
        loop(1, self.size, lambda d: act((self.me + d) % self.size))

    def start(self):
        self._each(lambda p: self._to(p).start())

    def wait_recv(self):
        self._each(lambda p: self._from(p).wait_recv())

    def wait_send(self):
        self._each(lambda p: self._from(p).wait_send())


class WeightGather:
    def __init__(self, g, h, s):
        self.g = g
        self.core = h % 2
        self.mate = h + 1 - 2 * self.core
        self.pair = h - self.core
        self.x, self.z = s // 8, s % 8

    def seq(self, x, z):
        return x * 8 + z

    def zz(self, d):
        return (self.z + d + 8) % 8

    def xx(self, d):
        return (self.x + d + 4) % 4

    def half(self, c):
        return self.g.w.at[:, pl.ds(pl.multiple_of(c * 64, 64), 64)]

    def arrived(self, x, z, src):
        slot = self.g.buf.at[x, z, src]
        remote(slot, slot, self.g.mate_send, self.g.wrecv.at[x, z, src], {"head": self.mate}).wait_recv()

    def forward(self, x, z, src, way, act):
        slot = self.g.buf.at[x, z, src]
        place = (
            self.seq(self.x, self.zz(1)), self.seq(self.x, self.zz(-1)),
            self.seq(self.xx(1), self.z), self.seq(self.xx(-1), self.z),
        )[way]
        copy = remote(slot, slot, self.g.wsend.at[way, x, z, src], self.g.wrecv.at[x, z, src], {"seq": place})
        act(copy)

    def sources(self, act):
        g, core = self.g, self.core
        dst = g.buf.at[self.x, self.z, core]
        act(remote(self.half(1 - core), dst, g.mate_send, g.wrecv.at[self.x, self.z, core], {"head": self.mate}))

        @pl.when(core == 0)
        def _():
            for d in (1, 3, 2):
                place = self.seq(self.xx(d), self.z)
                for c in range(2):
                    act(remote(self.half(c), g.buf.at[self.x, self.z, 0], g.first_send.at[d, c],
                               g.wrecv.at[self.x, self.z, 0], {"seq": place, "head": self.pair + c}))

        @pl.when(core == 1)
        def _():
            for d in (1, 3):
                place = self.seq(self.x, self.zz(1 if d == 1 else -1))
                for c in range(2):
                    act(remote(self.half(c), g.buf.at[self.x, self.z, 1], g.first_send.at[d, c],
                               g.wrecv.at[self.x, self.z, 1], {"seq": place, "head": self.pair + c}))

    def keep_own(self):
        self.g.buf[self.x, self.z, self.core] = self.g.w[:, pl.ds(pl.multiple_of(self.core * 64, 64), 64)]

    def round_z0(self, d, act):
        if d < 3:
            for i in range(4):
                self.forward(i, self.zz(-d), 0, 0, act)
                self.forward(i, self.zz(d), 0, 1, act)
        else:
            for i in range(2):
                self.forward(i, self.zz(-d), 0, 0, act)
                self.forward(i + 2, self.zz(d), 0, 1, act)

    def round_z1(self, d, act):
        self.forward(self.x, self.zz(-d), 1, 0, act)
        if d < 3:
            self.forward(self.x, self.zz(d), 1, 1, act)

    def round_x1(self, z, act):
        self.forward(self.x, z, 1, 2, act)
        self.forward(self.x, z, 1, 3, act)

    def turn_x1(self, z, act):
        even = z % 2 == 0

        @pl.when(even)
        def _():
            self.forward(self.xx(-1), z, 1, 2, act)

        @pl.when(jnp.logical_not(even))
        def _():
            self.forward(self.xx(1), z, 1, 3, act)

    def wait_z0(self, d):
        for i in range(4):
            self.arrived(i, self.zz(d), 0)

    def wait_sides(self, z):
        self.arrived(self.xx(1), z, 1)
        self.arrived(self.xx(-1), z, 1)

    def stage(self, number):
        begin = lambda copy: copy.start()
        if number == 0:
            self.sources(begin)
            self.keep_own()
        if number == 1:
            for d in (1, 2, 3):
                self.arrived(self.xx(d), self.z, 0)
            self.arrived(self.x, self.z, 1 - self.core)
            self.round_z0(0, begin)
            self.round_x1(self.z, begin)
            for d in (-1, 1):
                self.arrived(self.x, self.zz(d), 1)
            self.round_z1(1, begin)
            for d in (-1, 1):
                self.round_x1(self.zz(d), begin)
        if number == 2:
            for d in (-1, 1):
                self.wait_z0(d)
            self.round_z0(1, begin)
            for d in (-2, 2):
                self.arrived(self.x, self.zz(d), 1)
            self.round_z1(2, begin)
            for d in (0, -1, 1):
                self.wait_sides(self.zz(d))
                self.turn_x1(self.zz(d), begin)
            for d in (-2, 2):
                self.round_x1(self.zz(d), begin)
        if number == 3:
            for d in (-2, 2):
                self.wait_z0(d)
            self.round_z0(2, begin)
            for d in (-3, 3):
                self.arrived(self.x, self.zz(d), 1)
            self.round_z1(3, begin)
            for d in (-2, 2):
                self.wait_sides(self.zz(d))
                self.turn_x1(self.zz(d), begin)
            for d in (-3, 3):
                self.round_x1(self.zz(d), begin)
        if number == 4:
            for d in (-3, 3):
                self.wait_z0(d)
            self.round_z0(3, begin)
            self.arrived(self.x, self.zz(4), 1)
            self.round_x1(self.zz(4), begin)
            for d in (-3, 3):
                self.wait_sides(self.zz(d))
                self.turn_x1(self.zz(d), begin)
        if number == 5:
            self.wait_z0(4)
            self.wait_sides(self.zz(4))
            self.turn_x1(self.zz(4), begin)

    def far_side(self, z):
        self.arrived(self.xx(2), z, 1)

    def wait_send(self):
        done = lambda copy: copy.wait_send()
        self.sources(done)
        for d in range(4):
            self.round_z0(d, done)
        for d in (1, 2, 3):
            self.round_z1(d, done)
        for d in range(8):
            self.round_x1(self.zz(d), done)
            self.turn_x1(self.zz(d), done)


INPUTS = ("x", "mix", "down", "base", "up", "r", "k", "v", "dy", "u", "w", "mixes")
OUTPUTS = {
    "out": ((TOK, COL), BF16),
    "down_grad": ((COL, RANK), F32),
    "up_grad": ((RANK, COL), F32),
    "base_grad": ((1, COL), F32),
    "bonus_grad": ((1, COL), F32),
}
DMA = pltpu.SemaphoreType.DMA
SCRATCH = {
    "part1": pltpu.VMEM((N_HEAD, 8, 128), F32),
    "land1": pltpu.VMEM((N_HEAD, 8, 128), F32),
    "full1": pltpu.VMEM((N_HEAD, 8, 128), F32),
    "part2": pltpu.VMEM((N_HEAD, 8, 128), F32),
    "land2": pltpu.VMEM((N_HEAD, 8, 128), F32),
    "full2": pltpu.VMEM((N_HEAD, 8, 128), F32),
    "edge_part": pltpu.VMEM((8, 128), F32),
    "edge_land": pltpu.VMEM((N_HEAD, 8, 128), F32),
    "tail": pltpu.VMEM((16, COL), BF16),
    "pack": pltpu.VMEM((N_SEQ, 2, 8, 128), F32),
    "pack_in": pltpu.VMEM((N_SEQ, 2, 8, 128), F32),
    "back": pltpu.VMEM((N_SEQ, 8, 128), F32),
    "got": pltpu.VMEM((N_SEQ, 8, 128), F32),
    "pairs": pltpu.VMEM((8, TOK, COL), F32),
    "cross": pltpu.VMEM((4, TOK, 4 * TOK), BF16),
    "hold": pltpu.VMEM((8, TOK, COL), F32),
    "proj": pltpu.VMEM((2, 3, TOK, COL), BF16),
    "proj_edge": pltpu.VMEM((2, 3, 16, COL), BF16),
    "turned": pltpu.VMEM((2, 3, COL, 2 * TOK), BF16),
    "big": pltpu.VMEM((N_SEQ, 24, 128), F32),
    "big_in": pltpu.VMEM((N_SEQ, 24, 128), F32),
    "total": pltpu.VMEM((N_SEQ, 16, 128), F32),
    "gdi": pltpu.VMEM((TOK, COL), F32),
    "gdi_edge": pltpu.VMEM((8, COL), F32),
    "y_out": pltpu.VMEM((N_HEAD, 128, TOK), BF16),
    "y_in": pltpu.VMEM((N_HEAD, 128, TOK), BF16),
    "buf": pltpu.VMEM((4, 8, 2, 3, 64, COL), BF16),
    "h_sems": DMA((9, N_HEAD)),
    "y_sems": DMA((2, N_HEAD)),
    "s_sems": DMA((8, N_SEQ)),
    "one": DMA((11,)),
    "wrecv": DMA((4, 8, 2)),
    "wsend": DMA((4, 4, 8, 2)),
    "first_send": DMA((4, 2)),
    "mate_send": DMA,
}


def step_kernel(*refs):
    g = SimpleNamespace(**dict(zip((*INPUTS, *OUTPUTS, *SCRATCH), refs, strict=True)))
    h, s = lax.axis_index("head"), lax.axis_index("seq")
    core = h % 2
    mate = h + 1 - 2 * core
    nxt, prv = (s + 1) % N_SEQ, (s + N_SEQ - 1) % N_SEQ
    weights = WeightGather(g, h, s)

    barrier = pltpu.get_barrier_semaphore()
    loop(1, N_HEAD, lambda d: greet(barrier, {"head": (h + d) % N_HEAD}))

    def greet_seq(d):
        greet(barrier, {"seq": (s + d) % N_SEQ})
        greet(barrier, {"seq": (s + d) % N_SEQ, "head": mate})

    loop(1, N_SEQ, greet_seq)

    @pl.when(h == 0)
    def _():
        loop(0, N_HEAD, lambda j: greet(barrier, {"seq": prv, "head": j}))

    pl.semaphore_wait(barrier, N_HEAD - 1 + 2 * (N_SEQ - 1) + 1)

    row_copy = remote(g.x.at[pl.ds(TOK - 16, 16)], g.tail, g.one.at[0], g.one.at[1], {"seq": nxt})
    row_copy.start()
    x = g.x[...].astype(F32)
    mix = g.mix[...]
    down_h, down_l = parts(g.down[...], 2)

    def into_rank(a):
        a_h, a_l = parts(a, 2)
        return mm(a_h, down_h) + (mm(a_h, down_l) + mm(a_l, down_h))

    g.part1[...] = into_rank(shift_mix(x, 0.0, mix)).reshape(N_HEAD, 8, 128)
    in_first = AllToAll("head", N_HEAD, h, g.part1, g.land1, g.h_sems.at[0], g.h_sems.at[1])
    in_first.start()
    g.edge_part[...] = into_rank(mix * x[TOK - 8 :])
    edge_copy = remote(g.edge_part, g.edge_land.at[h], g.one.at[2], g.h_sems.at[4, h], {"seq": nxt, "head": 0})
    edge_copy.start()
    weights.stage(0)

    rb, kb, vb, dyb = g.r[...], g.k[...], g.v[...], g.dy[...]
    r, k, v, dy = (a.astype(F32) for a in (rb, kb, vb, dyb))
    u = g.u[...]
    own = block_diagonal()
    odd = odd_rows()
    lane_head = head_of(iota((TOK, COL), 1))
    heads = [lane_head == i for i in range(4)]
    zero16 = jnp.zeros((TOK, COL), BF16)

    def by_head(a):
        return jnp.concatenate([jnp.where(m, a, zero16) for m in heads], axis=0)

    def lane_cat(stacked):
        return jnp.concatenate([stacked[i * TOK : (i + 1) * TOK] for i in range(4)], axis=1)

    spread = jnp.where(own, 1.0, 0.0).astype(BF16)

    def tiles(a):
        return a.reshape(TOK // 8, 8, COL)

    def flat(a):
        return a.reshape(TOK, COL)

    for i, piece in enumerate(parts(mm(by_head(dyb), vb, LANES_LANES), 2)):
        g.cross[i] = lane_cat(piece)
    for i, piece in enumerate(parts(mm(by_head(vb), dyb, LANES_LANES), 2)):
        g.cross[2 + i] = lane_cat(piece)
    for d in range(8):
        v_old = v if d == 0 else flat(pltpu.roll(tiles(v), d, 1))
        g.pairs[d] = mm_right_exact(dy * v_old, spread)

    g.land1[h] = g.part1[h]
    in_first.wait_recv()

    @pl.when(h == 0)
    def _():
        def got_edge(j):
            remote(g.edge_part, g.edge_land.at[j], g.one.at[2], g.h_sems.at[4, j], {"seq": nxt}).wait_recv()

        loop(0, N_HEAD, got_edge)
        rows = g.edge_land[0]
        for j in range(1, N_HEAD):
            rows = rows + g.edge_land[j]
        first_row = jnp.where((iota((8, 128), 0) == 0) & (s > 0), pltpu.roll(rows, 1, 0), 0.0)
        g.land1[0] = g.land1[0] + first_row

    def summed(ref):
        acc = ref[0]
        for j in range(1, N_HEAD):
            acc = acc + ref[j]
        return acc

    g.full1[h] = summed(g.land1)
    in_second = AllToAll("head", N_HEAD, h, g.full1, g.full1, g.h_sems.at[2], g.h_sems.at[3], True)
    in_second.start()
    weights.stage(1)
    in_second.wait_recv()

    mid = jnp.tanh(g.full1[...].reshape(TOK, RANK))
    up_h, up_l = parts(g.up[...], 2)
    mid_h, mid_l = parts(mid, 2)
    w = -jnp.exp(g.base[...] + (mm(mid_h, up_h) + (mm(mid_h, up_l) + mm(mid_l, up_h))))
    w_parts = parts(w, 3)
    ones = lower_ones(False)
    cumul = mm(ones, w_parts[0]) + (mm(ones, w_parts[1]) + mm(ones, w_parts[2]))
    before = cumul - w
    final = cumul[TOK - 1 : TOK]
    all_ones = jnp.ones((TOK, 128), BF16)
    w_turned = [p.astype(F32).T.astype(BF16) for p in w_parts]
    total_rows = mm(w_turned[0], all_ones) + (mm(w_turned[1], all_ones) + mm(w_turned[2], all_ones))
    to_end = jnp.exp(jnp.minimum(final - cumul, 0.0))
    from_start = jnp.exp(before)

    def folded(a, b):
        wide = jnp.where(own, mm_right_exact(a.T, b), 0.0)
        return wide[:, :128] + wide[:, 128:]

    state = folded(k * to_end, vb)
    grad = folded(r * from_start, dyb)
    packed = jnp.where(odd, pltpu.roll(state, 64, 1), state) + jnp.where(odd, grad, pltpu.roll(grad, 64, 1))
    g.pack[:, 0] = packed.reshape(N_SEQ, 8, 128)
    g.pack[:, 1] = jnp.exp(total_rows).reshape(N_SEQ, 8, 128)
    to_owner = AllToAll("seq", N_SEQ, s, g.pack, g.pack_in, g.s_sems.at[0], g.s_sems.at[1])
    to_owner.start()
    g.pack_in[s] = g.pack[s]
    g.hold[0], g.hold[1], g.hold[2], g.hold[3] = w, cumul, to_end, from_start

    gr_mem = jnp.zeros((TOK, COL), F32)
    gk_in = jnp.zeros((TOK, COL), F32)
    score_st = jnp.zeros((4 * TOK, TOK), F32)
    tok = iota((TOK, COL), 0)

    def wide_mm(first, mask, factor):
        f_top, f_low = (by_head(p) for p in parts(factor, 2))
        zero = jnp.zeros((TOK, 4 * TOK), BF16)
        top, low = jnp.where(mask, g.cross[first], zero), jnp.where(mask, g.cross[first + 1], zero)
        return mm(top, f_top) + (mm(top, f_low) + mm(low, f_top))

    for half in (64, 32, 16, 8):
        size = 2 * half
        second = (tok % size) >= half
        middle = cumul.reshape(TOK // size, size, COL)[:, half - 1 : half]
        middle = jnp.broadcast_to(middle, (TOK // size, size, COL)).reshape(TOK, COL)
        fade = jnp.exp(jnp.minimum(jnp.where(second, before - middle, middle - cumul), 0.0))
        late, early = jnp.where(second, fade, 0.0), jnp.where(second, 0.0, fade)
        r_hat, k_hat = r * late, k * early
        same = iota((TOK, 4 * TOK), 0) // size == (iota((TOK, 4 * TOK), 1) % TOK) // size
        gr_mem = gr_mem + late * wide_mm(0, same, k_hat)
        gk_in = gk_in + early * wide_mm(2, same, r_hat)
        k_top, k_low = (by_head(p) for p in parts(k_hat, 2))
        r_top, r_low = parts(r_hat, 2)
        score = mm(k_top, r_top, LANES_LANES) + (mm(k_top, r_low, LANES_LANES) + mm(k_low, r_top, LANES_LANES))
        same_st = (iota((4 * TOK, TOK), 0) % TOK) // size == iota((4 * TOK, TOK), 1) // size
        score_st = score_st + jnp.where(same_st, score, 0.0)
    gv = jnp.zeros((TOK, COL), F32)
    dy_heads = by_head(dyb)
    for piece in parts(score_st, 2):
        gv = gv + mm(lane_cat(piece), dy_heads)

    to_owner.wait_recv()
    onward = jnp.zeros((8, 128), F32)
    forward = []
    for n in range(N_SEQ):
        forward.append(onward)
        onward = g.pack_in[n, 1] * onward + g.pack_in[n, 0]
    left8 = iota((8, 128), 1) < 64
    reverse = jnp.zeros((8, 128), F32)
    for n in reversed(range(N_SEQ)):
        g.back[n] = jnp.where(left8, forward[n], reverse)
        reverse = g.pack_in[n, 1] * reverse + g.pack_in[n, 0]
    to_range = AllToAll("seq", N_SEQ, s, g.back, g.got, g.s_sems.at[2], g.s_sems.at[3])
    to_range.start()
    g.got[s] = g.back[s]
    weights.stage(2)

    sub = iota((TOK // 8, 8, COL), 1)
    for d in range(1, 8):
        valid = sub >= d
        cum_old = pltpu.roll(tiles(cumul), d, 1)
        k_old = flat(pltpu.roll(tiles(k), d, 1))
        fade = jnp.exp(jnp.minimum(jnp.where(valid, tiles(before) - cum_old, 0.0), 0.0))
        fade = flat(jnp.where(valid, fade, 0.0))
        pair = g.pairs[d]
        faded_r = fade * r
        gr_mem = gr_mem + fade * pair * k_old
        gk_in = gk_in + flat(pltpu.roll(tiles(faded_r * pair), 8 - d, 1))
        score = mm_right_exact(faded_r * k_old, spread)
        gv = gv + flat(pltpu.roll(tiles(score * dy), 8 - d, 1))
    gv = gv + mm_right_exact(r * u * k, spread) * dy
    g.hold[4], g.hold[5], g.hold[6] = gr_mem, gk_in, gv
    to_range.wait_recv()

    w, cumul, to_end, from_start = g.hold[0], g.hold[1], g.hold[2], g.hold[3]
    packed = g.got[...].reshape(COL, 128)
    left = iota((COL, 128), 1) < 64
    state, grad = jnp.where(left, packed, 0.0), jnp.where(left, 0.0, packed)
    state = jnp.where(odd, pltpu.roll(state, 64, 1), state)
    grad = jnp.where(odd, grad, pltpu.roll(grad, 64, 1))
    state = jnp.where(own, jnp.concatenate([state, state], axis=1), 0.0)
    grad = jnp.where(own, jnp.concatenate([grad, grad], axis=1), 0.0)
    gr_mem = g.hold[4] + from_start * mm_left_exact(dyb, state, LANES_LANES)
    gk_in = g.hold[5]
    gk_out = to_end * mm_left_exact(vb, grad, LANES_LANES)
    across = mm_left_exact(jnp.ones((8, COL), BF16), state * grad, LANES_LANES, 3)[0:1]
    across = across * jnp.exp(cumul[TOK - 1 : TOK])
    k_in = k * gk_in
    g_log = across - k_in + mm_left_exact(lower_ones(True), k * gk_out)
    g_log = g_log + mm_left_exact(upper_ones(), r * gr_mem - k_in)
    g_pre = g_log * w
    g.part2[...] = mm3(g_pre, g.up[...], LANES_LANES).reshape(N_HEAD, 8, 128)
    out_first = AllToAll("head", N_HEAD, h, g.part2, g.land2, g.h_sems.at[5], g.h_sems.at[6])
    out_first.start()
    g.land2[h] = g.part2[h]

    self_pair = g.pairs[0]
    r_pair = r * self_pair
    g.proj[core, 0] = (gr_mem + u * k * self_pair).astype(BF16)
    g.proj[core, 1] = (gk_in + gk_out + u * r_pair).astype(BF16)
    g.proj[core, 2] = (g.hold[6] + mm3(k * to_end, grad)).astype(BF16)
    swap = remote(g.proj.at[core], g.proj.at[core], g.one.at[3], g.one.at[4], {"head": mate})
    first_rows = g.proj.at[core, :, pl.ds(0, 16)]
    near = remote(first_rows, g.proj_edge.at[core], g.one.at[5], g.one.at[6], {"seq": prv})
    far = remote(first_rows, g.proj_edge.at[core], g.one.at[7], g.one.at[8], {"seq": prv, "head": mate})
    swap.start()
    near.start()
    far.start()
    weights.stage(3)
    raising = mm3(mid.T, g_pre)
    g.big[16:24, 0:16] = raising[:, 0:128].reshape(8, 16, 128)
    g.big[24:32, 0:16] = raising[:, 128:256].reshape(8, 16, 128)
    floor_row = jnp.sum(g_pre, axis=0, keepdims=True)
    bonus_row = jnp.sum(k * r_pair, axis=0, keepdims=True)
    row8 = iota((8, 128), 0)
    small = jnp.where(row8 == 0, floor_row[:, :128], 0.0) + jnp.where(row8 == 1, floor_row[:, 128:], 0.0)
    small = small + jnp.where(row8 == 2, bonus_row[:, :128], 0.0) + jnp.where(row8 == 3, bonus_row[:, 128:], 0.0)
    g.big[:, 16:24] = jnp.broadcast_to(small[None], (N_SEQ, 8, 128))
    row_copy.wait()
    carried = jnp.where(s == 0, 0.0, g.tail[...].astype(F32)[15:16])
    turned_in = shift_mix(x, carried, mix).T

    out_first.wait_recv()
    g.full2[h] = summed(g.land2)
    out_second = AllToAll("head", N_HEAD, h, g.full2, g.full2, g.h_sems.at[7], g.h_sems.at[8], True)
    out_second.start()

    swap.wait()
    near.wait()
    far.wait()
    for c in range(2):
        for m in range(3):
            a = g.proj[c, m].astype(F32)
            edge = jnp.where(s == N_SEQ - 1, 0.0, g.proj_edge[c, m].astype(F32)[0:1])
            later = jnp.where(tok == TOK - 1, edge, pltpu.roll(a, TOK - 1, 0))
            g.turned[c, m, :, 0:TOK] = a.T.astype(BF16)
            g.turned[c, m, :, TOK:] = later.T.astype(BF16)
    out_second.wait_recv()

    g_mid = g.full2[...].reshape(TOK, RANK) * (1.0 - mid * mid)
    g.big[0:16, 0:16] = mm3(turned_in, g_mid).reshape(16, 16, 128)
    sums_first = AllToAll("seq", N_SEQ, s, g.big, g.big_in, g.s_sems.at[4], g.s_sems.at[5])
    gdi = mm3(g_mid, g.down[...], LANES_LANES)
    g.gdi[...] = gdi
    edge_row = remote(g.gdi.at[pl.ds(0, 8)], g.gdi_edge, g.one.at[9], g.one.at[10], {"seq": prv})
    weights.stage(4)
    sums_first.start()
    edge_row.start()
    g.big_in[s] = g.big[s]

    def y_send(to):
        return remote(g.y_out.at[to], g.y_in.at[h], g.y_sems.at[0, to], g.y_sems.at[1, h], {"head": to})

    def y_from(frm):
        return remote(g.y_out.at[frm], g.y_in.at[frm], g.y_sems.at[0, frm], g.y_sems.at[1, frm], {"head": frm})

    near_pair = (s % 8) // 2
    for turn in (0, 1, 3, 2):
        pair = (near_pair + turn) % 4
        if turn == 2:
            weights.stage(5)
        weights.far_side(2 * pair)
        weights.far_side(2 * pair + 1)
        mixes = g.mixes[pair].T
        acc = jnp.zeros((4 * TOK, TOK), F32)
        for m in range(3):
            term = None
            for c in range(2):
                rows = g.buf[:, pl.ds(2 * pair, 2), c, m].reshape(4 * TOK, COL)
                one = mm(rows, g.turned[c, m])
                term = one if term is None else term + one
            here, there = term[:, :TOK], term[:, TOK:]
            acc = acc + here + mixes[:, m : m + 1] * (there - here)
        for i in range(4):
            to = 4 * i + pair
            g.y_out[to] = acc[i * TOK : (i + 1) * TOK].astype(BF16)

            @pl.when(to != h)
            def _():
                y_send(to).start()

    sums_first.wait_recv()
    acc = g.big_in[0]
    for n in range(1, N_SEQ):
        acc = acc + g.big_in[n]
    g.total[s] = acc[:16]
    sums_second = AllToAll("seq", N_SEQ, s, g.total, g.total, g.s_sems.at[6], g.s_sems.at[7], True)
    sums_second.start()
    g.base_grad[:, 0:128] = acc[16:17]
    g.base_grad[:, 128:256] = acc[17:18]
    g.bonus_grad[:, 0:128] = acc[18:19]
    g.bonus_grad[:, 128:256] = acc[19:20]

    edge_row.wait()
    gdi = g.gdi[...]
    next_row = jnp.where(s == N_SEQ - 1, 0.0, g.gdi_edge[0:1])
    later = jnp.where(tok == TOK - 1, next_row, pltpu.roll(gdi, TOK - 1, 0))
    mine = gdi + mix * (later - gdi)
    g.y_in[h] = g.y_out[h]
    loop(1, N_HEAD, lambda d: y_from((h + d) % N_HEAD).wait_recv())
    halves = []
    for c in range(2):
        acc = g.y_in[c].astype(F32)
        for y in range(1, 8):
            acc = acc + g.y_in[2 * y + c].astype(F32)
        halves.append(acc)
    lo, hi = halves
    joined = jnp.concatenate([lo[:64], hi[:64], lo[64:], hi[64:]], axis=0)
    g.out[...] = (joined.T + mine).astype(BF16)

    sums_second.wait_recv()
    g.down_grad[...] = g.total[0:16].reshape(COL, RANK)
    g.up_grad[:, 0:128] = g.total[16:24].reshape(RANK, 128)
    g.up_grad[:, 128:256] = g.total[24:32].reshape(RANK, 128)

    edge_copy.wait_send()
    for copies in (in_first, in_second, out_first, out_second, to_owner, to_range, sums_first, sums_second):
        copies.wait_send()
    loop(1, N_HEAD, lambda d: y_from((h + d) % N_HEAD).wait_send())
    weights.wait_send()


def step(*operands):
    return pl.pallas_call(
        step_kernel,
        out_shape=tuple(jax.ShapeDtypeStruct(*spec) for spec in OUTPUTS.values()),
        in_specs=[VMEM] * len(INPUTS),
        out_specs=(VMEM,) * len(OUTPUTS),
        scratch_shapes=list(SCRATCH.values()),
        compiler_params=pltpu.CompilerParams(
            collective_id=0, has_side_effects=True, vmem_limit_bytes=60 * 2**20
        ),
        name="step",
    )(*operands)


def per_device(
    layer_input, receptance, key_act, value_act, attention_result_sensitivity, time_first,
    decay_exponent_base, decay_shift_mix, mix_rkv, decay_adapter_down, decay_adapter_up, proj_weights,
):
    core = lax.axis_index("head") % 2
    mixes = lax.dynamic_index_in_dim(mix_rkv.reshape(3, 4, 4, 2, 2, 64), core, 4, keepdims=False)
    mixes = jnp.moveaxis(mixes, 2, 0).reshape(4, 3, 512)
    mixes = jnp.pad(mixes, ((0, 0), (0, 5), (0, 0)))
    out, down_grad, up_grad, base_grad, bonus_grad = step(
        layer_input, decay_shift_mix[None], decay_adapter_down, decay_exponent_base[None], decay_adapter_up,
        receptance, key_act, value_act, attention_result_sensitivity, time_first.reshape(1, COL),
        proj_weights, mixes,
    )
    return out, down_grad, up_grad, base_grad.reshape(COL), bonus_grad.reshape(4, HS)


def solution(mesh):
    return jax.shard_map(
        per_device,
        mesh=mesh,
        in_specs=(
            P("seq", "head"), P("seq", "head"), P("seq", "head"), P("seq", "head"), P("seq", "head"),
            P("head", None), P("head"), P("head"), P(), P("head", None), P(None, "head"),
            P(None, "seq", "head"),
        ),
        out_specs=(P("seq", "head"), P("head", None), P(None, "head"), P("head"), P("head", None)),
        check_vma=False,
    )
```

time: 594 us -> 115 us (0.19)
  local copies, waits for them, and re-layouts: 199 us -> 7.3 us
  waiting for transfers between devices: 168 us -> 0 us
  Pallas kernels: 0 us -> 105 us
  blocking collectives: 61.8 us -> 0 us
  other arithmetic: 62.2 us -> 1.33 us
  matrix products: 54.1 us -> 0 us
  starting transfers between devices: 26.4 us -> 0 us
  between operations: 14.8 us -> 0.7 us
    gather x194 -> x0, local copies, waits for them, and re-layouts: 129 us -> none
    pallas_call x0 -> x1, Pallas kernels: none -> 105 us  [step(): pl.pallas_call(step_kernel, out_shape=tuple((jax.ShapeDtypeStruct(*spec)...]
    psum x1 -> x0, waiting for transfers between devices: 93.5 us -> none  [per_device(): lax.psum((down_local, device_raising_matrix, device_fading_floor, device_...]
    psum x1 -> x0, blocking collectives: 61.8 us -> none  [per_device(): lax.psum((down_local, device_raising_matrix, device_fading_floor, device_...]
    all_gather x5 -> x0, waiting for transfers between devices: 59.7 us -> none  [the longest x2 59.7 us: gathered_total(): return lax.all_gather(array, axis).sum(0)]
    dot_general x44 -> x0, matrix products: 54.1 us -> none  [the longest x4 17.9 us: sensitivity_each_segment(): jnp.einsum('tshi,thi,shi->tsh', decays, gate_matrix, lookup_matrix, preci...]
    while x8 -> x0, other arithmetic: 22.7 us -> none
    all_to_all x2 -> x0, starting transfers between devices: 15.3 us -> none  [the longest x1 10.5 us: sent_to_all(): return lax.all_to_all(copies, axis, split_axis=0, concat_axis=0, tiled=True)]
  transfers between devices with their start and end apart: 10 -> 0, of which waited for: 5 -> 0; matrix products, arithmetic and copies ran while one was open for 48% -> 0% of each run, Pallas kernels for 0% -> 0%
where the time goes in v2:
time: 115 us; the launch traced here: 114 us
  Pallas kernels  105 us (91%)
  local copies, waits for them, and re-layouts  7.3 us (6%)
  other arithmetic  1.33 us (1%)
    pallas_call x1, Pallas kernels, step(): pl.pallas_call(step_kernel, out_shape=tuple((jax.ShapeDtypeStruct(*spec)...  105 us
    unnamed x12, local copies, waits for them, and re-layouts  3.69 us

profile of v2, /device:TPU:6, one launch (start us, length us, event | category | flops | bytes accessed | tf_op | source)
XLA Modules:
  0.0 113.9 jit_solution(11293423236527778916)
XLA Ops:
  0.6 1.0 reshape.26
  1.6 0.1 constant_dynamic-slice_fusion
  1.7 0.1 reshape.27
  1.8 0.0 copy-start.2
  1.8 0.6 pad.4.refs_11_
  2.5 0.0 copy-done.2
  2.5 0.6 reshape.25.refs_9_
  3.2 104.6 %step.1 = (bf16[128,256]{1,0:T(8,128)(2,1)}, f32[256,128]{1,0:T(8,128)}, f32[128,256]{1,0:T(8,128)}, f32[1,256]{1,0:T(1,128)}, f32[1,256]{1,0:T(1,128)}) custom-call(bf16[128,256]{1,0:T(8,128)(2,1)} %refs_0_.1, f32[1,256]{1,0:T(1,128)} %bitcast.11, f32[256,128]{1,0:T(8,128)} %refs_2_.1, f32[1,256]{1,0:T(1,128)} %bitcast.12, f32[128,256]{1,0:T(8,128)} %refs_4_.1, ...), custom_call_target="tpu_custom_call" | custom-call | tf_op jit(solution)/shard_map/step/pallas_call | solution.py:693
  107.8 0.0 copy-start.1
  107.8 0.5 broadcast.6
  108.3 1.3 %reduce.3 = f32[256]{0:T(256)S(1)} reduce(f32[1,256]{1,0:T(1,128)} %get-tuple-element.14, f32[]{:T(128)} %broadcast.6), dimensions={0}, to_apply=%get-tuple-element.14.reduce_sub_computation.3 | reduce | bytes 2052 | tf_op jit(solution)/shard_map/step/pallas_call | solution.py:693
  109.6 0.7 reshape.29
  110.3 1.5 %copy.26 = bf16[128,256]{1,0:T(8,128)(2,1)} copy(bf16[128,256]{1,0:T(8,128)(2,1)} %get-tuple-element.20) | data formatting | bytes 131072
  111.7 0.0 copy-done.1
  111.7 0.0 copy-start
  111.7 0.7 copy.27
  112.4 0.3 copy-done
  112.7 0.0 copy-start.3
  112.7 0.7 copy.28
  113.3 0.0 copy-done.3
  113.4 0.6 copy.29
  (2 shorter events, 0.0 us)
Async XLA Ops:
  1.8 0.7 copy-start.2
  107.8 4.0 %copy-start.1 = (f32[256,128]{1,0:T(8,128)S(1)}, f32[256,128]{1,0:T(8,128)}, u32[]{:S(2)}) copy-start(f32[256,128]{1,0:T(8,128)} %get-tuple-element.21) | copy-start | bytes 393220
  111.7 1.0 copy-start
  112.7 0.7 copy-start.3

commit v3 on v2

--- a/solution.py
+++ b/solution.py
@@ -111,29 +111,27 @@
 
 
 class AllToAll:
-    def __init__(self, axis, size, me, out, land, send, recv, broadcast=False):
+    def __init__(self, axis, size, me, out, land, sems, number, broadcast=False):
         self.axis, self.size, self.me = axis, size, me
-        self.out, self.land, self.send, self.recv, self.broadcast = out, land, send, recv, broadcast
-
-    def _to(self, peer):
+        self.out, self.land, self.broadcast = out, land, broadcast
+        self.send, self.recv = sems.at[number, 0], sems.at[number, 1]
+
+    def start_one(self, peer):
         src = self.out.at[self.me if self.broadcast else peer]
-        return remote(src, self.land.at[self.me], self.send.at[peer], self.recv.at[self.me], {self.axis: peer})
-
-    def _from(self, peer):
-        src = self.out.at[self.me if self.broadcast else peer]
-        return remote(src, self.land.at[peer], self.send.at[peer], self.recv.at[peer], {self.axis: peer})
-
-    def _each(self, act):
-        loop(1, self.size, lambda d: act((self.me + d) % self.size))
+        remote(src, self.land.at[self.me], self.send, self.recv, {self.axis: peer}).start()
 
     def start(self):
-        self._each(lambda p: self._to(p).start())
+        loop(1, self.size, lambda d: self.start_one((self.me + d) % self.size))
+
+    def _all(self):
+        others = self.land.at[pl.ds(0, self.size - 1)]
+        return remote(others, others, self.send, self.recv, {self.axis: (self.me + 1) % self.size})
 
     def wait_recv(self):
-        self._each(lambda p: self._from(p).wait_recv())
+        self._all().wait_recv()
 
     def wait_send(self):
-        self._each(lambda p: self._from(p).wait_send())
+        self._all().wait_send()
 
 
 class WeightGather:
@@ -156,160 +154,174 @@
     def half(self, c):
         return self.g.w.at[:, pl.ds(pl.multiple_of(c * 64, 64), 64)]
 
-    def arrived(self, x, z, src):
-        slot = self.g.buf.at[x, z, src]
-        remote(slot, slot, self.g.mate_send, self.g.wrecv.at[x, z, src], {"head": self.mate}).wait_recv()
-
-    def forward(self, x, z, src, way, act):
-        slot = self.g.buf.at[x, z, src]
+    def land(self, x, z, src, kind):
+        return self.g.buf.at[x, z, src], self.g.wrecv.at[kind, z]
+
+    def arrived(self, blocks, z, kind):
+        send = self.g.mate_send
+        remote(blocks, blocks, send, self.g.wrecv.at[kind, z], {"head": self.mate}).wait_recv()
+
+    def forward(self, x, z, src, way, kind, group):
+        slot, sem = self.land(x, z, src, kind)
         place = (
             self.seq(self.x, self.zz(1)), self.seq(self.x, self.zz(-1)),
             self.seq(self.xx(1), self.z), self.seq(self.xx(-1), self.z),
         )[way]
-        copy = remote(slot, slot, self.g.wsend.at[way, x, z, src], self.g.wrecv.at[x, z, src], {"seq": place})
-        act(copy)
+        remote(slot, slot, self.g.wsend.at[group], sem, {"seq": place}).start()
 
     def sources(self, act):
         g, core = self.g, self.core
         dst = g.buf.at[self.x, self.z, core]
-        act(remote(self.half(1 - core), dst, g.mate_send, g.wrecv.at[self.x, self.z, core], {"head": self.mate}))
+        act(remote(self.half(1 - core), dst, g.mate_send, g.mate_recv, {"head": self.mate}))
 
         @pl.when(core == 0)
         def _():
+            dst, sem = self.land(self.x, self.z, 0, 0)
             for d in (1, 3, 2):
                 place = self.seq(self.xx(d), self.z)
                 for c in range(2):
-                    act(remote(self.half(c), g.buf.at[self.x, self.z, 0], g.first_send.at[d, c],
-                               g.wrecv.at[self.x, self.z, 0], {"seq": place, "head": self.pair + c}))
+                    act(remote(self.half(c), dst, g.first_send.at[d, c], sem, {"seq": place, "head": self.pair + c}))
 
         @pl.when(core == 1)
         def _():
+            dst, sem = self.land(self.x, self.z, 1, 1)
             for d in (1, 3):
                 place = self.seq(self.x, self.zz(1 if d == 1 else -1))
                 for c in range(2):
-                    act(remote(self.half(c), g.buf.at[self.x, self.z, 1], g.first_send.at[d, c],
-                               g.wrecv.at[self.x, self.z, 1], {"seq": place, "head": self.pair + c}))
+                    act(remote(self.half(c), dst, g.first_send.at[d, c], sem, {"seq": place, "head": self.pair + c}))
 
     def keep_own(self):
         self.g.buf[self.x, self.z, self.core] = self.g.w[:, pl.ds(pl.multiple_of(self.core * 64, 64), 64)]
 
-    def round_z0(self, d, act):
+    def round_z0(self, d):
+        for i in range(4 if d < 3 else 2):
+            self.forward(i, self.zz(-d), 0, 0, 0, 0 if d < 3 else 2)
+            self.forward(i if d < 3 else i + 2, self.zz(d), 0, 1, 0, 0 if d < 3 else 2)
+
+    def round_z1(self, d):
+        self.forward(self.x, self.zz(-d), 1, 0, 1, 2 if d < 3 else 3)
         if d < 3:
-            for i in range(4):
-                self.forward(i, self.zz(-d), 0, 0, act)
-                self.forward(i, self.zz(d), 0, 1, act)
-        else:
-            for i in range(2):
-                self.forward(i, self.zz(-d), 0, 0, act)
-                self.forward(i + 2, self.zz(d), 0, 1, act)
-
-    def round_z1(self, d, act):
-        self.forward(self.x, self.zz(-d), 1, 0, act)
-        if d < 3:
-            self.forward(self.x, self.zz(d), 1, 1, act)
-
-    def round_x1(self, z, act):
-        self.forward(self.x, z, 1, 2, act)
-        self.forward(self.x, z, 1, 3, act)
-
-    def turn_x1(self, z, act):
+            self.forward(self.x, self.zz(d), 1, 1, 1, 2)
+
+    def round_x1(self, d):
+        z = self.zz(d)
+        self.forward(self.x, z, 1, 2, 2, 1)
+        self.forward(self.x, z, 1, 3, 2, 1)
+
+    def turn_x1(self, d):
+        z = self.zz(d)
         even = z % 2 == 0
 
         @pl.when(even)
         def _():
-            self.forward(self.xx(-1), z, 1, 2, act)
+            self.forward(self.xx(-1), z, 1, 2, 3, 0)
 
         @pl.when(jnp.logical_not(even))
         def _():
-            self.forward(self.xx(1), z, 1, 3, act)
+            self.forward(self.xx(1), z, 1, 3, 3, 0)
 
     def wait_z0(self, d):
-        for i in range(4):
-            self.arrived(i, self.zz(d), 0)
-
-    def wait_sides(self, z):
-        self.arrived(self.xx(1), z, 1)
-        self.arrived(self.xx(-1), z, 1)
+        z = self.zz(d)
+        self.arrived(self.g.buf.at[:, z, 0], z, 0)
+
+    def wait_own(self, d):
+        z = self.zz(d)
+        self.arrived(self.g.buf.at[self.x, z, 1], z, 1)
+
+    def wait_sides(self, d):
+        z = self.zz(d)
+        self.arrived(self.g.buf.at[pl.ds(0, 2), z, 1], z, 2)
 
     def stage(self, number):
-        begin = lambda copy: copy.start()
+        g = self.g
         if number == 0:
-            self.sources(begin)
-            self.keep_own()
+            self.sources(lambda copy: copy.start())
         if number == 1:
-            for d in (1, 2, 3):
-                self.arrived(self.xx(d), self.z, 0)
-            self.arrived(self.x, self.z, 1 - self.core)
-            self.round_z0(0, begin)
-            self.round_x1(self.z, begin)
+            self.arrived(g.buf.at[pl.ds(0, 3), self.z, 0], self.z, 0)
+            slot = g.buf.at[self.x, self.z, 1 - self.core]
+            remote(slot, slot, g.mate_send, g.mate_recv, {"head": self.mate}).wait_recv()
+            self.round_z0(0)
+            self.round_x1(0)
             for d in (-1, 1):
-                self.arrived(self.x, self.zz(d), 1)
-            self.round_z1(1, begin)
+                self.wait_own(d)
+            self.round_z1(1)
             for d in (-1, 1):
-                self.round_x1(self.zz(d), begin)
+                self.round_x1(d)
         if number == 2:
             for d in (-1, 1):
                 self.wait_z0(d)
-            self.round_z0(1, begin)
+            self.round_z0(1)
             for d in (-2, 2):
-                self.arrived(self.x, self.zz(d), 1)
-            self.round_z1(2, begin)
+                self.wait_own(d)
+            self.round_z1(2)
             for d in (0, -1, 1):
-                self.wait_sides(self.zz(d))
-                self.turn_x1(self.zz(d), begin)
+                self.wait_sides(d)
+                self.turn_x1(d)
             for d in (-2, 2):
-                self.round_x1(self.zz(d), begin)
+                self.round_x1(d)
         if number == 3:
             for d in (-2, 2):
                 self.wait_z0(d)
-            self.round_z0(2, begin)
+            self.round_z0(2)
             for d in (-3, 3):
-                self.arrived(self.x, self.zz(d), 1)
-            self.round_z1(3, begin)
+                self.wait_own(d)
+            self.round_z1(3)
             for d in (-2, 2):
-                self.wait_sides(self.zz(d))
-                self.turn_x1(self.zz(d), begin)
+                self.wait_sides(d)
+                self.turn_x1(d)
             for d in (-3, 3):
-                self.round_x1(self.zz(d), begin)
+                self.round_x1(d)
         if number == 4:
             for d in (-3, 3):
                 self.wait_z0(d)
-            self.round_z0(3, begin)
-            self.arrived(self.x, self.zz(4), 1)
-            self.round_x1(self.zz(4), begin)
+            self.round_z0(3)
+            self.wait_own(4)
+            self.round_x1(4)
             for d in (-3, 3):
-                self.wait_sides(self.zz(d))
-                self.turn_x1(self.zz(d), begin)
+                self.wait_sides(d)
+                self.turn_x1(d)
         if number == 5:
             self.wait_z0(4)
-            self.wait_sides(self.zz(4))
-            self.turn_x1(self.zz(4), begin)
+            self.wait_sides(4)
+            self.turn_x1(4)
 
     def far_side(self, z):
-        self.arrived(self.xx(2), z, 1)
+        self.arrived(self.g.buf.at[self.xx(2), z, 1], z, 3)
 
     def wait_send(self):
-        done = lambda copy: copy.wait_send()
-        self.sources(done)
-        for d in range(4):
-            self.round_z0(d, done)
-        for d in (1, 2, 3):
-            self.round_z1(d, done)
-        for d in range(8):
-            self.round_x1(self.zz(d), done)
-            self.turn_x1(self.zz(d), done)
-
-
-INPUTS = ("x", "mix", "down", "base", "up", "r", "k", "v", "dy", "u", "w", "mixes")
+        g = self.g
+        self.sources(lambda copy: copy.wait_send())
+        waited = (g.buf.at[pl.ds(0, 2)], g.buf.at[0], g.buf.at[0, pl.ds(0, 4)], g.buf.at[0, 0, 0])
+        for group, blocks in enumerate(waited):
+            remote(blocks, blocks, g.wsend.at[group], g.mate_recv, {"head": self.mate}).wait_send()
+
+
+INPUTS = {
+    "x": ((TOK, COL), BF16),
+    "mix": ((1, COL), F32),
+    "down": ((COL, RANK), F32),
+    "dy": ((TOK, COL), BF16),
+    "v": ((TOK, COL), BF16),
+    "w": ((3, TOK, COL), BF16),
+    "base": ((1, COL), F32),
+    "up": ((RANK, COL), F32),
+    "r": ((TOK, COL), BF16),
+    "k": ((TOK, COL), BF16),
+    "u": ((4, HS), F32),
+    "mixes": ((3, 4096), F32),
+}
 OUTPUTS = {
     "out": ((TOK, COL), BF16),
     "down_grad": ((COL, RANK), F32),
     "up_grad": ((RANK, COL), F32),
     "base_grad": ((1, COL), F32),
-    "bonus_grad": ((1, COL), F32),
+    "bonus_grad": ((8, HS), F32),
 }
 DMA = pltpu.SemaphoreType.DMA
 SCRATCH = {
+    **{name: pltpu.VMEM(*spec) for name, spec in INPUTS.items()},
+    "in_sems": DMA((len(INPUTS),)),
+    "mix_columns": pltpu.VMEM((4, 4 * TOK, 3), F32),
     "part1": pltpu.VMEM((N_HEAD, 8, 128), F32),
     "land1": pltpu.VMEM((N_HEAD, 8, 128), F32),
     "full1": pltpu.VMEM((N_HEAD, 8, 128), F32),
@@ -329,27 +341,36 @@
     "proj": pltpu.VMEM((2, 3, TOK, COL), BF16),
     "proj_edge": pltpu.VMEM((2, 3, 16, COL), BF16),
     "turned": pltpu.VMEM((2, 3, COL, 2 * TOK), BF16),
-    "big": pltpu.VMEM((N_SEQ, 24, 128), F32),
-    "big_in": pltpu.VMEM((N_SEQ, 24, 128), F32),
-    "total": pltpu.VMEM((N_SEQ, 16, 128), F32),
+    "rise": pltpu.VMEM((N_SEQ, 16, 128), F32),
+    "rise_in": pltpu.VMEM((N_SEQ, 16, 128), F32),
+    "rise_total": pltpu.VMEM((N_SEQ, 8, 128), F32),
+    "fall": pltpu.VMEM((N_SEQ, 8, 128), F32),
+    "fall_in": pltpu.VMEM((N_SEQ, 8, 128), F32),
+    "fall_total": pltpu.VMEM((N_SEQ, 8, 128), F32),
     "gdi": pltpu.VMEM((TOK, COL), F32),
     "gdi_edge": pltpu.VMEM((8, COL), F32),
     "y_out": pltpu.VMEM((N_HEAD, 128, TOK), BF16),
     "y_in": pltpu.VMEM((N_HEAD, 128, TOK), BF16),
     "buf": pltpu.VMEM((4, 8, 2, 3, 64, COL), BF16),
-    "h_sems": DMA((9, N_HEAD)),
-    "y_sems": DMA((2, N_HEAD)),
-    "s_sems": DMA((8, N_SEQ)),
-    "one": DMA((11,)),
-    "wrecv": DMA((4, 8, 2)),
-    "wsend": DMA((4, 4, 8, 2)),
+    "pair_sems": DMA((11, 2)),
+    "one": DMA((12,)),
+    "wrecv": DMA((4, 8)),
+    "mate_recv": DMA,
+    "wsend": DMA((4,)),
     "first_send": DMA((4, 2)),
     "mate_send": DMA,
 }
 
 
 def step_kernel(*refs):
-    g = SimpleNamespace(**dict(zip((*INPUTS, *OUTPUTS, *SCRATCH), refs, strict=True)))
+    given, refs = refs[: len(INPUTS)], refs[len(INPUTS) :]
+    g = SimpleNamespace(**dict(zip((*OUTPUTS, *SCRATCH), refs, strict=True)))
+    fetches = {
+        name: pltpu.make_async_copy(ref, getattr(g, name), g.in_sems.at[i])
+        for i, (name, ref) in enumerate(zip(INPUTS, given, strict=True))
+    }
+    for fetch in fetches.values():
+        fetch.start()
     h, s = lax.axis_index("head"), lax.axis_index("seq")
     core = h % 2
     mate = h + 1 - 2 * core
@@ -369,10 +390,11 @@
     def _():
         loop(0, N_HEAD, lambda j: greet(barrier, {"seq": prv, "head": j}))
 
-    pl.semaphore_wait(barrier, N_HEAD - 1 + 2 * (N_SEQ - 1) + 1)
-
-    row_copy = remote(g.x.at[pl.ds(TOK - 16, 16)], g.tail, g.one.at[0], g.one.at[1], {"seq": nxt})
-    row_copy.start()
+    def fetched(*names):
+        for name in names:
+            fetches[name].wait()
+
+    fetched("x", "mix", "down")
     x = g.x[...].astype(F32)
     mix = g.mix[...]
     down_h, down_l = parts(g.down[...], 2)
@@ -382,16 +404,22 @@
         return mm(a_h, down_h) + (mm(a_h, down_l) + mm(a_l, down_h))
 
     g.part1[...] = into_rank(shift_mix(x, 0.0, mix)).reshape(N_HEAD, 8, 128)
-    in_first = AllToAll("head", N_HEAD, h, g.part1, g.land1, g.h_sems.at[0], g.h_sems.at[1])
+    g.edge_part[...] = into_rank(mix * x[TOK - 8 :])
+    g.land1[h] = g.part1[h]
+    fetched("w")
+    weights.keep_own()
+    fetched("dy", "v", "r", "k", "u", "base", "up", "mixes")
+    pl.semaphore_wait(barrier, N_HEAD - 1 + 2 * (N_SEQ - 1) + 1)
+    in_first = AllToAll("head", N_HEAD, h, g.part1, g.land1, g.pair_sems, 0)
     in_first.start()
-    g.edge_part[...] = into_rank(mix * x[TOK - 8 :])
-    edge_copy = remote(g.edge_part, g.edge_land.at[h], g.one.at[2], g.h_sems.at[4, h], {"seq": nxt, "head": 0})
+    edge_copy = remote(g.edge_part, g.edge_land.at[h], g.one.at[2], g.one.at[11], {"seq": nxt, "head": 0})
     edge_copy.start()
     weights.stage(0)
+    row_copy = remote(g.x.at[pl.ds(TOK - 16, 16)], g.tail, g.one.at[0], g.one.at[1], {"seq": nxt})
+    row_copy.start()
 
     rb, kb, vb, dyb = g.r[...], g.k[...], g.v[...], g.dy[...]
     r, k, v, dy = (a.astype(F32) for a in (rb, kb, vb, dyb))
-    u = g.u[...]
     own = block_diagonal()
     odd = odd_rows()
     lane_head = head_of(iota((TOK, COL), 1))
@@ -405,6 +433,10 @@
         return jnp.concatenate([stacked[i * TOK : (i + 1) * TOK] for i in range(4)], axis=1)
 
     spread = jnp.where(own, 1.0, 0.0).astype(BF16)
+    unfold = jnp.where(iota((HS, COL), 0) == iota((HS, COL), 1) % HS, 1.0, 0.0).astype(BF16)
+    head_rows = iota((8, COL), 0) == head_of(iota((8, COL), 1))
+    u = jnp.concatenate([g.u[...], jnp.zeros((4, HS), F32)], axis=0)
+    u = jnp.sum(jnp.where(head_rows, mm_right_exact(u, unfold, count=3), 0.0), axis=0, keepdims=True)
 
     def tiles(a):
         return a.reshape(TOK // 8, 8, COL)
@@ -420,15 +452,11 @@
         v_old = v if d == 0 else flat(pltpu.roll(tiles(v), d, 1))
         g.pairs[d] = mm_right_exact(dy * v_old, spread)
 
-    g.land1[h] = g.part1[h]
     in_first.wait_recv()
 
     @pl.when(h == 0)
     def _():
-        def got_edge(j):
-            remote(g.edge_part, g.edge_land.at[j], g.one.at[2], g.h_sems.at[4, j], {"seq": nxt}).wait_recv()
-
-        loop(0, N_HEAD, got_edge)
+        remote(g.edge_land, g.edge_land, g.one.at[2], g.one.at[11], {"seq": nxt}).wait_recv()
         rows = g.edge_land[0]
         for j in range(1, N_HEAD):
             rows = rows + g.edge_land[j]
@@ -442,7 +470,7 @@
         return acc
 
     g.full1[h] = summed(g.land1)
-    in_second = AllToAll("head", N_HEAD, h, g.full1, g.full1, g.h_sems.at[2], g.h_sems.at[3], True)
+    in_second = AllToAll("head", N_HEAD, h, g.full1, g.full1, g.pair_sems, 1, True)
     in_second.start()
     weights.stage(1)
     in_second.wait_recv()
@@ -471,7 +499,7 @@
     packed = jnp.where(odd, pltpu.roll(state, 64, 1), state) + jnp.where(odd, grad, pltpu.roll(grad, 64, 1))
     g.pack[:, 0] = packed.reshape(N_SEQ, 8, 128)
     g.pack[:, 1] = jnp.exp(total_rows).reshape(N_SEQ, 8, 128)
-    to_owner = AllToAll("seq", N_SEQ, s, g.pack, g.pack_in, g.s_sems.at[0], g.s_sems.at[1])
+    to_owner = AllToAll("seq", N_SEQ, s, g.pack, g.pack_in, g.pair_sems, 4)
     to_owner.start()
     g.pack_in[s] = g.pack[s]
     g.hold[0], g.hold[1], g.hold[2], g.hold[3] = w, cumul, to_end, from_start
@@ -508,6 +536,7 @@
     for piece in parts(score_st, 2):
         gv = gv + mm(lane_cat(piece), dy_heads)
 
+    weights.stage(2)
     to_owner.wait_recv()
     onward = jnp.zeros((8, 128), F32)
     forward = []
@@ -519,10 +548,9 @@
     for n in reversed(range(N_SEQ)):
         g.back[n] = jnp.where(left8, forward[n], reverse)
         reverse = g.pack_in[n, 1] * reverse + g.pack_in[n, 0]
-    to_range = AllToAll("seq", N_SEQ, s, g.back, g.got, g.s_sems.at[2], g.s_sems.at[3])
+    to_range = AllToAll("seq", N_SEQ, s, g.back, g.got, g.pair_sems, 5)
     to_range.start()
     g.got[s] = g.back[s]
-    weights.stage(2)
 
     sub = iota((TOK // 8, 8, COL), 1)
     for d in range(1, 8):
@@ -539,6 +567,7 @@
         gv = gv + flat(pltpu.roll(tiles(score * dy), 8 - d, 1))
     gv = gv + mm_right_exact(r * u * k, spread) * dy
     g.hold[4], g.hold[5], g.hold[6] = gr_mem, gk_in, gv
+    weights.stage(3)
     to_range.wait_recv()
 
     w, cumul, to_end, from_start = g.hold[0], g.hold[1], g.hold[2], g.hold[3]
@@ -559,7 +588,7 @@
     g_log = g_log + mm_left_exact(upper_ones(), r * gr_mem - k_in)
     g_pre = g_log * w
     g.part2[...] = mm3(g_pre, g.up[...], LANES_LANES).reshape(N_HEAD, 8, 128)
-    out_first = AllToAll("head", N_HEAD, h, g.part2, g.land2, g.h_sems.at[5], g.h_sems.at[6])
+    out_first = AllToAll("head", N_HEAD, h, g.part2, g.land2, g.pair_sems, 2)
     out_first.start()
     g.land2[h] = g.part2[h]
 
@@ -575,24 +604,27 @@
     swap.start()
     near.start()
     far.start()
-    weights.stage(3)
     raising = mm3(mid.T, g_pre)
-    g.big[16:24, 0:16] = raising[:, 0:128].reshape(8, 16, 128)
-    g.big[24:32, 0:16] = raising[:, 128:256].reshape(8, 16, 128)
+    g.rise[0:16, 0:8] = raising[:, 0:128].reshape(16, 8, 128)
+    g.rise[16:32, 0:8] = raising[:, 128:256].reshape(16, 8, 128)
     floor_row = jnp.sum(g_pre, axis=0, keepdims=True)
     bonus_row = jnp.sum(k * r_pair, axis=0, keepdims=True)
     row8 = iota((8, 128), 0)
     small = jnp.where(row8 == 0, floor_row[:, :128], 0.0) + jnp.where(row8 == 1, floor_row[:, 128:], 0.0)
     small = small + jnp.where(row8 == 2, bonus_row[:, :128], 0.0) + jnp.where(row8 == 3, bonus_row[:, 128:], 0.0)
-    g.big[:, 16:24] = jnp.broadcast_to(small[None], (N_SEQ, 8, 128))
+    g.rise[:, 8:16] = jnp.broadcast_to(small[None], (N_SEQ, 8, 128))
+    rise_first = AllToAll("seq", N_SEQ, s, g.rise, g.rise_in, g.pair_sems, 6)
+    rise_first.start()
+    g.rise_in[s] = g.rise[s]
     row_copy.wait()
     carried = jnp.where(s == 0, 0.0, g.tail[...].astype(F32)[15:16])
     turned_in = shift_mix(x, carried, mix).T
 
     out_first.wait_recv()
     g.full2[h] = summed(g.land2)
-    out_second = AllToAll("head", N_HEAD, h, g.full2, g.full2, g.h_sems.at[7], g.h_sems.at[8], True)
+    out_second = AllToAll("head", N_HEAD, h, g.full2, g.full2, g.pair_sems, 3, True)
     out_second.start()
+    weights.stage(4)
 
     swap.wait()
     near.wait()
@@ -604,25 +636,33 @@
             later = jnp.where(tok == TOK - 1, edge, pltpu.roll(a, TOK - 1, 0))
             g.turned[c, m, :, 0:TOK] = a.T.astype(BF16)
             g.turned[c, m, :, TOK:] = later.T.astype(BF16)
+    for pair in range(4):
+        columns = []
+        for i in range(4):
+            for p in range(2):
+                place = 8 * i + 2 * pair + p
+                column = g.mixes[:, place * 128 : (place + 1) * 128].T
+                columns.append(jnp.where(core == 0, column[:64], column[64:]))
+        g.mix_columns[pair] = jnp.concatenate(columns, axis=0)
     out_second.wait_recv()
 
     g_mid = g.full2[...].reshape(TOK, RANK) * (1.0 - mid * mid)
-    g.big[0:16, 0:16] = mm3(turned_in, g_mid).reshape(16, 16, 128)
-    sums_first = AllToAll("seq", N_SEQ, s, g.big, g.big_in, g.s_sems.at[4], g.s_sems.at[5])
+    g.fall[...] = mm3(turned_in, g_mid).reshape(N_SEQ, 8, 128)
+    fall_first = AllToAll("seq", N_SEQ, s, g.fall, g.fall_in, g.pair_sems, 7)
+    fall_first.start()
     gdi = mm3(g_mid, g.down[...], LANES_LANES)
     g.gdi[...] = gdi
     edge_row = remote(g.gdi.at[pl.ds(0, 8)], g.gdi_edge, g.one.at[9], g.one.at[10], {"seq": prv})
-    weights.stage(4)
-    sums_first.start()
     edge_row.start()
-    g.big_in[s] = g.big[s]
-
-    def y_send(to):
-        return remote(g.y_out.at[to], g.y_in.at[h], g.y_sems.at[0, to], g.y_sems.at[1, h], {"head": to})
-
-    def y_from(frm):
-        return remote(g.y_out.at[frm], g.y_in.at[frm], g.y_sems.at[0, frm], g.y_sems.at[1, frm], {"head": frm})
-
+    g.fall_in[s] = g.fall[s]
+
+    def summed_seq(ref):
+        acc = ref[0]
+        for n in range(1, N_SEQ):
+            acc = acc + ref[n]
+        return acc
+
+    y_copy = AllToAll("head", N_HEAD, h, g.y_out, g.y_in, g.pair_sems, 10)
     near_pair = (s % 8) // 2
     for turn in (0, 1, 3, 2):
         pair = (near_pair + turn) % 4
@@ -630,7 +670,7 @@
             weights.stage(5)
         weights.far_side(2 * pair)
         weights.far_side(2 * pair + 1)
-        mixes = g.mixes[pair].T
+        mixes = g.mix_columns[pair]
         acc = jnp.zeros((4 * TOK, TOK), F32)
         for m in range(3):
             term = None
@@ -646,19 +686,27 @@
 
             @pl.when(to != h)
             def _():
-                y_send(to).start()
-
-    sums_first.wait_recv()
-    acc = g.big_in[0]
-    for n in range(1, N_SEQ):
-        acc = acc + g.big_in[n]
-    g.total[s] = acc[:16]
-    sums_second = AllToAll("seq", N_SEQ, s, g.total, g.total, g.s_sems.at[6], g.s_sems.at[7], True)
-    sums_second.start()
-    g.base_grad[:, 0:128] = acc[16:17]
-    g.base_grad[:, 128:256] = acc[17:18]
-    g.bonus_grad[:, 0:128] = acc[18:19]
-    g.bonus_grad[:, 128:256] = acc[19:20]
+                y_copy.start_one(to)
+
+        if turn == 0:
+            rise_first.wait_recv()
+            acc = summed_seq(g.rise_in)
+            g.rise_total[s] = acc[:8]
+            rise_second = AllToAll("seq", N_SEQ, s, g.rise_total, g.rise_total, g.pair_sems, 8, True)
+            rise_second.start()
+            g.base_grad[:, 0:128] = acc[8:9]
+            g.base_grad[:, 128:256] = acc[9:10]
+            bonus = jnp.concatenate([acc[10:11], acc[11:12]], axis=1)
+            bonus = jnp.where(head_rows, bonus, 0.0)
+            rows = None
+            for piece in parts(bonus, 3):
+                one = mm(piece, unfold, LANES_LANES)
+                rows = one if rows is None else rows + one
+            g.bonus_grad[...] = rows
+    fall_first.wait_recv()
+    g.fall_total[s] = summed_seq(g.fall_in)
+    fall_second = AllToAll("seq", N_SEQ, s, g.fall_total, g.fall_total, g.pair_sems, 9, True)
+    fall_second.start()
 
     edge_row.wait()
     gdi = g.gdi[...]
@@ -666,7 +714,7 @@
     later = jnp.where(tok == TOK - 1, next_row, pltpu.roll(gdi, TOK - 1, 0))
     mine = gdi + mix * (later - gdi)
     g.y_in[h] = g.y_out[h]
-    loop(1, N_HEAD, lambda d: y_from((h + d) % N_HEAD).wait_recv())
+    y_copy.wait_recv()
     halves = []
     for c in range(2):
         acc = g.y_in[c].astype(F32)
@@ -677,23 +725,25 @@
     joined = jnp.concatenate([lo[:64], hi[:64], lo[64:], hi[64:]], axis=0)
     g.out[...] = (joined.T + mine).astype(BF16)
 
-    sums_second.wait_recv()
-    g.down_grad[...] = g.total[0:16].reshape(COL, RANK)
-    g.up_grad[:, 0:128] = g.total[16:24].reshape(RANK, 128)
-    g.up_grad[:, 128:256] = g.total[24:32].reshape(RANK, 128)
-
     edge_copy.wait_send()
-    for copies in (in_first, in_second, out_first, out_second, to_owner, to_range, sums_first, sums_second):
+    for copies in (
+        in_first, in_second, out_first, out_second, to_owner, to_range, rise_first, rise_second, fall_first, y_copy,
+    ):
         copies.wait_send()
-    loop(1, N_HEAD, lambda d: y_from((h + d) % N_HEAD).wait_send())
     weights.wait_send()
+    rise_second.wait_recv()
+    g.up_grad[:, 0:128] = g.rise_total[0:16].reshape(RANK, 128)
+    g.up_grad[:, 128:256] = g.rise_total[16:32].reshape(RANK, 128)
+    fall_second.wait_recv()
+    g.down_grad[...] = g.fall_total[...].reshape(COL, RANK)
+    fall_second.wait_send()
 
 
 def step(*operands):
     return pl.pallas_call(
         step_kernel,
         out_shape=tuple(jax.ShapeDtypeStruct(*spec) for spec in OUTPUTS.values()),
-        in_specs=[VMEM] * len(INPUTS),
+        in_specs=[pl.BlockSpec(memory_space=pl.ANY)] * len(INPUTS),
         out_specs=(VMEM,) * len(OUTPUTS),
         scratch_shapes=list(SCRATCH.values()),
         compiler_params=pltpu.CompilerParams(
@@ -703,20 +753,38 @@
     )(*operands)
 
 
+def finish_kernel(out_in, down_in, up_in, base_in, bonus_in, out, down_grad, up_grad, base_grad, bonus_grad):
+    out[...] = out_in[...]
+    down_grad[...] = down_in[...]
+    up_grad[...] = up_in[...]
+    base_grad[...] = base_in[...].reshape(COL)
+    bonus_grad[...] = bonus_in[0:4]
+
+
+def finish(*results):
+    return pl.pallas_call(
+        finish_kernel,
+        out_shape=(
+            *(jax.ShapeDtypeStruct(*spec) for spec in list(OUTPUTS.values())[:3]),
+            jax.ShapeDtypeStruct((COL,), F32),
+            jax.ShapeDtypeStruct((4, HS), F32),
+        ),
+        in_specs=[VMEM] * 5,
+        out_specs=(VMEM,) * 5,
+        name="finish",
+    )(*results)
+
+
 def per_device(
     layer_input, receptance, key_act, value_act, attention_result_sensitivity, time_first,
     decay_exponent_base, decay_shift_mix, mix_rkv, decay_adapter_down, decay_adapter_up, proj_weights,
 ):
-    core = lax.axis_index("head") % 2
-    mixes = lax.dynamic_index_in_dim(mix_rkv.reshape(3, 4, 4, 2, 2, 64), core, 4, keepdims=False)
-    mixes = jnp.moveaxis(mixes, 2, 0).reshape(4, 3, 512)
-    mixes = jnp.pad(mixes, ((0, 0), (0, 5), (0, 0)))
-    out, down_grad, up_grad, base_grad, bonus_grad = step(
-        layer_input, decay_shift_mix[None], decay_adapter_down, decay_exponent_base[None], decay_adapter_up,
-        receptance, key_act, value_act, attention_result_sensitivity, time_first.reshape(1, COL),
-        proj_weights, mixes,
-    )
-    return out, down_grad, up_grad, base_grad.reshape(COL), bonus_grad.reshape(4, HS)
+    given = {
+        "x": layer_input, "mix": decay_shift_mix[None], "down": decay_adapter_down,
+        "base": decay_exponent_base[None], "up": decay_adapter_up, "r": receptance, "k": key_act,
+        "v": value_act, "dy": attention_result_sensitivity, "u": time_first, "w": proj_weights, "mixes": mix_rkv,
+    }
+    return finish(*step(*(given[name] for name in INPUTS)))
 
 
 def solution(mesh):

time: 115 us -> 92 us (0.80)
  Pallas kernels: 105 us -> 91.2 us
  local copies, waits for them, and re-layouts: 7.3 us -> 0 us
  other arithmetic: 1.33 us -> 0 us
    pallas_call x1, Pallas kernels: 105 us -> 89.5 us  [step(): pl.pallas_call(step_kernel, out_shape=tuple((jax.ShapeDtypeStruct(*spec)...]
    unnamed x12 -> x0, local copies, waits for them, and re-layouts: 3.69 us -> none
    reshape x5 -> x0, local copies, waits for them, and re-layouts: 2.39 us -> none  [the longest x1 0.97 us: per_device(): mix_rkv.reshape(3, 4, 4, 2, 2, 64)]
    pallas_call x0 -> x1, Pallas kernels: none -> 1.74 us  [finish(): pl.pallas_call(finish_kernel, out_shape=(*(jax.ShapeDtypeStruct(*spec) fo...]
    pallas_call x1 -> x0, other arithmetic: 1.33 us -> none  [step(): pl.pallas_call(step_kernel, out_shape=tuple((jax.ShapeDtypeStruct(*spec)...]
where the time goes in v3:
time: 92 us; the launch traced here: 91.9 us
  Pallas kernels  91.2 us (99%)
    pallas_call x1, Pallas kernels, step(): pl.pallas_call(step_kernel, out_shape=tuple((jax.ShapeDtypeStruct(*spec)...  89.5 us

profile of v3, /device:TPU:6, one launch (start us, length us, event | category | flops | bytes accessed | tf_op | source)
XLA Modules:
  0.0 91.9 jit_solution(16985848274567552775)
XLA Ops:
  0.6 89.5 %step.1 = (bf16[128,256]{1,0:T(8,128)(2,1)}, f32[256,128]{1,0:T(8,128)}, f32[128,256]{1,0:T(8,128)}, f32[1,256]{1,0:T(1,128)}, f32[8,64]{1,0:T(8,128)}) custom-call(bf16[128,256]{1,0:T(8,128)(2,1)} %refs_0_.1, f32[1,256]{1,0:T(1,128)} %bitcast.2, f32[256,128]{1,0:T(8,128)} %refs_2_.1, bf16[128,256]{1,0:T(8,128)(2,1)} %refs_3_.1, bf16[128,256]{1,0:T(8,128)(2,1)} %refs_4_.1, ...), custom_call_target="tpu_custom_call" | custom-call | tf_op jit(solution)/shard_map/step/pallas_call | solution.py:743
  90.1 1.7 %finish.1 = (bf16[128,256]{1,0:T(8,128)(2,1)}, f32[256,128]{1,0:T(8,128)}, f32[128,256]{1,0:T(8,128)}, f32[256]{0:T(256)}, f32[4,64]{1,0:T(4,128)}) custom-call(bf16[128,256]{1,0:T(8,128)(2,1)} %get-tuple-element.10.out_in, f32[256,128]{1,0:T(8,128)} %get-tuple-element.11.down_in, f32[128,256]{1,0:T(8,128)} %get-tuple-element.12.up_in, ...), custom_call_target="tpu_custom_call" | custom-call | tf_op jit(solution)/shard_map/finish/pallas_call | solution.py:765

commit v4 on v3

--- a/solution.py
+++ b/solution.py
@@ -155,11 +155,11 @@
         return self.g.w.at[:, pl.ds(pl.multiple_of(c * 64, 64), 64)]
 
     def land(self, x, z, src, kind):
-        return self.g.buf.at[x, z, src], self.g.wrecv.at[kind, z]
+        return self.g.buf.at[x, z, src], self.g.zrecv.at[x, z] if kind == 0 else self.g.wrecv.at[kind - 1, z]
 
     def arrived(self, blocks, z, kind):
         send = self.g.mate_send
-        remote(blocks, blocks, send, self.g.wrecv.at[kind, z], {"head": self.mate}).wait_recv()
+        remote(blocks, blocks, send, self.g.wrecv.at[kind - 1, z], {"head": self.mate}).wait_recv()
 
     def forward(self, x, z, src, way, kind, group):
         slot, sem = self.land(x, z, src, kind)
@@ -193,10 +193,23 @@
     def keep_own(self):
         self.g.buf[self.x, self.z, self.core] = self.g.w[:, pl.ds(pl.multiple_of(self.core * 64, 64), 64)]
 
+    def wait_z0(self, j, d):
+        slot, sem = self.land(self.xx(j), self.zz(d), 0, 0)
+        remote(slot, slot, self.g.mate_send, sem, {"head": self.mate}).wait_recv()
+
     def round_z0(self, d):
-        for i in range(4 if d < 3 else 2):
-            self.forward(i, self.zz(-d), 0, 0, 0, 0 if d < 3 else 2)
-            self.forward(i if d < 3 else i + 2, self.zz(d), 0, 1, 0, 0 if d < 3 else 2)
+        for j in (0, 1, 3, 2):
+            up, down = d < 3 or j in (0, 1), d < 3 or j in (3, 2)
+            if d == 0 and j != 0:
+                self.wait_z0(j, 0)
+            if d > 0:
+                self.wait_z0(j, -d)
+            if up:
+                self.forward(self.xx(j), self.zz(-d), 0, 0, 0, 0 if d < 3 else 2)
+            if d > 0:
+                self.wait_z0(j, d)
+            if down:
+                self.forward(self.xx(j), self.zz(d), 0, 1, 0, 0 if d < 3 else 2)
 
     def round_z1(self, d):
         self.forward(self.x, self.zz(-d), 1, 0, 1, 2 if d < 3 else 3)
@@ -219,10 +232,6 @@
         @pl.when(jnp.logical_not(even))
         def _():
             self.forward(self.xx(1), z, 1, 3, 3, 0)
-
-    def wait_z0(self, d):
-        z = self.zz(d)
-        self.arrived(self.g.buf.at[:, z, 0], z, 0)
 
     def wait_own(self, d):
         z = self.zz(d)
@@ -237,20 +246,16 @@
         if number == 0:
             self.sources(lambda copy: copy.start())
         if number == 1:
-            self.arrived(g.buf.at[pl.ds(0, 3), self.z, 0], self.z, 0)
             slot = g.buf.at[self.x, self.z, 1 - self.core]
             remote(slot, slot, g.mate_send, g.mate_recv, {"head": self.mate}).wait_recv()
-            self.round_z0(0)
             self.round_x1(0)
             for d in (-1, 1):
                 self.wait_own(d)
             self.round_z1(1)
             for d in (-1, 1):
                 self.round_x1(d)
+            self.round_z0(0)
         if number == 2:
-            for d in (-1, 1):
-                self.wait_z0(d)
-            self.round_z0(1)
             for d in (-2, 2):
                 self.wait_own(d)
             self.round_z1(2)
@@ -259,10 +264,8 @@
                 self.turn_x1(d)
             for d in (-2, 2):
                 self.round_x1(d)
+            self.round_z0(1)
         if number == 3:
-            for d in (-2, 2):
-                self.wait_z0(d)
-            self.round_z0(2)
             for d in (-3, 3):
                 self.wait_own(d)
             self.round_z1(3)
@@ -271,19 +274,20 @@
                 self.turn_x1(d)
             for d in (-3, 3):
                 self.round_x1(d)
+            self.round_z0(2)
         if number == 4:
-            for d in (-3, 3):
-                self.wait_z0(d)
-            self.round_z0(3)
             self.wait_own(4)
             self.round_x1(4)
             for d in (-3, 3):
                 self.wait_sides(d)
                 self.turn_x1(d)
+            self.round_z0(3)
         if number == 5:
-            self.wait_z0(4)
             self.wait_sides(4)
             self.turn_x1(4)
+        if number == 6:
+            for j in (0, 1, 3, 2):
+                self.wait_z0(j, 4)
 
     def far_side(self, z):
         self.arrived(self.g.buf.at[self.xx(2), z, 1], z, 3)
@@ -354,7 +358,8 @@
     "buf": pltpu.VMEM((4, 8, 2, 3, 64, COL), BF16),
     "pair_sems": DMA((11, 2)),
     "one": DMA((12,)),
-    "wrecv": DMA((4, 8)),
+    "zrecv": DMA((4, 8)),
+    "wrecv": DMA((3, 8)),
     "mate_recv": DMA,
     "wsend": DMA((4,)),
     "first_send": DMA((4, 2)),
@@ -666,8 +671,14 @@
     near_pair = (s % 8) // 2
     for turn in (0, 1, 3, 2):
         pair = (near_pair + turn) % 4
+        if turn == 1:
+            weights.stage(5)
         if turn == 2:
-            weights.stage(5)
+            fall_first.wait_recv()
+            g.fall_total[s] = summed_seq(g.fall_in)
+            fall_second = AllToAll("seq", N_SEQ, s, g.fall_total, g.fall_total, g.pair_sems, 9, True)
+            fall_second.start()
+            weights.stage(6)
         weights.far_side(2 * pair)
         weights.far_side(2 * pair + 1)
         mixes = g.mix_columns[pair]
@@ -703,10 +714,6 @@
                 one = mm(piece, unfold, LANES_LANES)
                 rows = one if rows is None else rows + one
             g.bonus_grad[...] = rows
-    fall_first.wait_recv()
-    g.fall_total[s] = summed_seq(g.fall_in)
-    fall_second = AllToAll("seq", N_SEQ, s, g.fall_total, g.fall_total, g.pair_sems, 9, True)
-    fall_second.start()
 
     edge_row.wait()
     gdi = g.gdi[...]

time: 92 us -> 90.7 us (0.986)
  Pallas kernels: 91.2 us -> 89.1 us
    pallas_call x1, Pallas kernels: 89.5 us -> 87.4 us  [step(): pl.pallas_call(step_kernel, out_shape=tuple((jax.ShapeDtypeStruct(*spec)...]
where the time goes in v4:
time: 90.7 us; the launch traced here: 89.8 us
  Pallas kernels  89.1 us (98%)
    pallas_call x1, Pallas kernels, step(): pl.pallas_call(step_kernel, out_shape=tuple((jax.ShapeDtypeStruct(*spec)...  87.4 us

profile of v4, /device:TPU:6, one launch (start us, length us, event | category | flops | bytes accessed | tf_op | source)
XLA Modules:
  0.0 89.8 jit_solution(9383125623262982822)
XLA Ops:
  0.6 87.4 %step.1 = (bf16[128,256]{1,0:T(8,128)(2,1)}, f32[256,128]{1,0:T(8,128)}, f32[128,256]{1,0:T(8,128)}, f32[1,256]{1,0:T(1,128)}, f32[8,64]{1,0:T(8,128)}) custom-call(bf16[128,256]{1,0:T(8,128)(2,1)} %refs_0_.1, f32[1,256]{1,0:T(1,128)} %bitcast.2, f32[256,128]{1,0:T(8,128)} %refs_2_.1, bf16[128,256]{1,0:T(8,128)(2,1)} %refs_3_.1, bf16[128,256]{1,0:T(8,128)(2,1)} %refs_4_.1, ...), custom_call_target="tpu_custom_call" | custom-call | tf_op jit(solution)/shard_map/step/pallas_call | solution.py:750
  88.0 1.7 %finish.1 = (bf16[128,256]{1,0:T(8,128)(2,1)}, f32[256,128]{1,0:T(8,128)}, f32[128,256]{1,0:T(8,128)}, f32[256]{0:T(256)}, f32[4,64]{1,0:T(4,128)}) custom-call(bf16[128,256]{1,0:T(8,128)(2,1)} %get-tuple-element.10.out_in, f32[256,128]{1,0:T(8,128)} %get-tuple-element.11.down_in, f32[128,256]{1,0:T(8,128)} %get-tuple-element.12.up_in, ...), custom_call_target="tpu_custom_call" | custom-call | tf_op jit(solution)/shard_map/finish/pallas_call | solution.py:772
